TPU v7x, 32 devices: a whole 2x2x4 slice. The times are simulated.
32 devices in a mesh: groups: 2 (over x), grid: 4 (over y, core), orb: 4 (over z).
Axes of the slice: x: 2, y: 2, z: 4, core: 2. Of those that a mesh axis runs over, the one named last changes fastest.
Arguments:
- orbitals: float32 [32, 2, 128, 128, 128], P(('groups', 'orb'), None, 'grid'), parts along dimension 0, may hold values from -6 to 6
- v_local: float32 [256, 128, 128], P(('groups', 'grid')), parts along dimension 0, may hold values from -24 to 24
- occupations: float32 [32], P('groups'), parts along dimension 0, may hold values from 0.05 to 0.5
Outputs:
- orbitals_next: float32 [32, 2, 128, 128, 128], P(('groups', 'orb'), None, 'grid'), parts along dimension 0
There are 2 independent parts, one for each index of `groups`. A program takes and returns all parts, laid end to end along the dimension named above; each array names one. Nothing has to cross between parts.
All inputs are finite; a program needn't handle non-finite values.
Results may differ from a plain program's by a relative error of at most 0.00035.
Values sent between devices are 32-bit elements; how exact they have to be, the bound alone decides.
A program may use at most 128 MiB of HBM per device.

v0:
```python
from functools import partial
import math

import jax
import jax.numpy as jnp
import ml_dtypes
import numpy as np
from jax import lax
from jax.experimental import pallas as pl
from jax.experimental.pallas import tpu as pltpu
from jax.sharding import PartitionSpec as P

TIME_STEP = 0.05
KINETIC_RATE = 0.1
HARTREE_SCALE = math.pi
HIGHEST = lax.Precision.HIGHEST
VMEM_LIMIT = 50 * 1024 * 1024


def wave_squared(length):
    ids = np.arange(length)
    signed = np.where(ids < (length + 1) // 2, ids, ids - length)
    return (2.0 * np.pi * signed / length) ** 2


def fourier(length, sign):
    ids = np.arange(length)
    return np.exp(sign * 2j * np.pi * ((ids[:, None] * ids[None, :]) % length) / length)


def kinetic_matrix(length):
    phase = np.exp(-1j * KINETIC_RATE * wave_squared(length))
    return (fourier(length, 1) / length * phase[None, :]) @ fourier(length, -1)


def left_block(matrix):
    return np.block([[matrix.real, -matrix.imag], [matrix.imag, matrix.real]])


def right_block(matrix):
    return np.block([[matrix.real, matrix.imag], [-matrix.imag, matrix.real]])


def split_const(table):
    table = np.asarray(table, np.float32)
    high = table.astype(ml_dtypes.bfloat16)
    low = (table - high.astype(np.float32)).astype(ml_dtypes.bfloat16)
    return np.stack([high, low])


def split(values):
    high = values.astype(jnp.bfloat16)
    low = (values - high.astype(jnp.float32)).astype(jnp.bfloat16)
    return high, low


def dot(left, right):
    return jnp.dot(left, right, preferred_element_type=jnp.float32)


def data_by_table(values, table):
    high, low = split(values)
    return dot(high, table[0]) + dot(high, table[1]) + dot(low, table[0])


def table_by_data(table, values):
    high, low = split(values)
    return dot(table[0], high) + dot(table[1], high) + dot(table[0], low)


def local_kernel(psi_ref, wz_ref, wy_ref, out_ref):
    _, _, bx, ny, nz = psi_ref.shape
    grid_count, _, _, vy, _ = out_ref.shape
    real_part = psi_ref[0, 0].reshape(bx * ny, nz)
    imag_part = psi_ref[0, 1].reshape(bx * ny, nz)
    turned = data_by_table(jnp.concatenate([real_part, imag_part], 1), wz_ref)
    columns = [
        jnp.concatenate(
            [turned[p * ny : (p + 1) * ny, :nz], turned[p * ny : (p + 1) * ny, nz:]], 0
        )
        for p in range(bx)
    ]
    rows = table_by_data(wy_ref, jnp.concatenate(columns, 1))
    for g in range(grid_count):
        for c in range(2):
            start = c * ny + g * vy
            for p in range(bx):
                out_ref[g, c, p] = rows[start : start + vy, p * nz : (p + 1) * nz]


def kinetic_local(orbitals, layer, grid_count, wz, wy):
    _, _, planes, ny, nz = orbitals.shape
    bx = min(4, planes)
    vy = ny // grid_count
    return pl.pallas_call(
        local_kernel,
        grid=(planes // bx,),
        in_specs=[
            pl.BlockSpec((1, 2, bx, ny, nz), lambda i: (layer, 0, i, 0, 0)),
            pl.BlockSpec(wz.shape, lambda i: (0, 0, 0)),
            pl.BlockSpec(wy.shape, lambda i: (0, 0, 0)),
        ],
        out_specs=pl.BlockSpec((grid_count, 2, bx, vy, nz), lambda i: (0, 0, i, 0, 0)),
        out_shape=jax.ShapeDtypeStruct((grid_count, 2, planes, vy, nz), jnp.float32),
        compiler_params=pltpu.CompilerParams(vmem_limit_bytes=VMEM_LIMIT),
        cost_estimate=pl.CostEstimate(
            flops=3 * 8 * planes * ny * nz * (ny + nz),
            bytes_accessed=16 * planes * ny * nz,
            transcendentals=0,
        ),
    )(orbitals, wz, wy)


def across_kernel(planes, first, weight_ref, psi_ref, wx_ref, *refs):
    if first:
        out_ref, density_ref = refs
    else:
        earlier_ref, out_ref, density_ref = refs
    depth, by, nz = psi_ref.shape
    columns = jnp.concatenate([psi_ref[:, j, :] for j in range(by)], 1)
    moved = table_by_data(wx_ref, columns)
    squares = moved * moved
    weight = weight_ref[0]
    for j in range(by):
        out_ref[:, j, :] = moved[:, j * nz : (j + 1) * nz]
    for h in range(depth // (2 * planes)):
        low = 2 * h * planes
        term = weight * (squares[low : low + planes] + squares[low + planes : low + 2 * planes])
        for j in range(by):
            value = term[:, j * nz : (j + 1) * nz]
            if not first:
                value = value + earlier_ref[h * planes : (h + 1) * planes, j, :]
            density_ref[h * planes : (h + 1) * planes, j, :] = value


def kinetic_across(received, weight, density, wx):
    grid_count, _, planes, vy, nz = received.shape
    depth = grid_count * 2 * planes
    by = min(8, vy)
    first = density is None
    block = pl.BlockSpec((depth, by, nz), lambda i: (0, i, 0))
    density_block = pl.BlockSpec((depth // 2, by, nz), lambda i: (0, i, 0))
    in_specs = [
        pl.BlockSpec(memory_space=pltpu.SMEM),
        block,
        pl.BlockSpec(wx.shape, lambda i: (0, 0, 0)),
    ]
    operands = [weight, received.reshape(depth, vy, nz), wx]
    if not first:
        in_specs.append(density_block)
        operands.append(density)
    moved, density = pl.pallas_call(
        partial(across_kernel, planes, first),
        grid=(vy // by,),
        in_specs=in_specs,
        out_specs=[block, density_block],
        out_shape=[
            jax.ShapeDtypeStruct((depth, vy, nz), jnp.float32),
            jax.ShapeDtypeStruct((depth // 2, vy, nz), jnp.float32),
        ],
        compiler_params=pltpu.CompilerParams(vmem_limit_bytes=VMEM_LIMIT),
        cost_estimate=pl.CostEstimate(
            flops=3 * 2 * depth * depth * vy * nz,
            bytes_accessed=12 * depth * vy * nz,
            transcendentals=0,
        ),
    )(*operands)
    return moved.reshape(grid_count, 2, planes, vy, nz), density


def rotate_kernel(layers, *refs):
    cos_ref, sin_ref = refs[layers], refs[layers + 1]
    out_ref = refs[layers + 2]
    grid_count, _, _, vy, _ = refs[0].shape
    for g in range(grid_count):
        band = slice(g * vy, (g + 1) * vy)
        cosine = cos_ref[:, band, :]
        sine = sin_ref[:, band, :]
        for l in range(layers):
            real_part = refs[l][g, 0]
            imag_part = refs[l][g, 1]
            out_ref[l, 0, :, band, :] = real_part * cosine + imag_part * sine
            out_ref[l, 1, :, band, :] = imag_part * cosine - real_part * sine


def rotate(returned, cosine, sine):
    layers = len(returned)
    grid_count, _, planes, vy, nz = returned[0].shape
    ny = grid_count * vy
    bx = min(4, planes)
    field_block = pl.BlockSpec((bx, ny, nz), lambda i: (i, 0, 0))
    return pl.pallas_call(
        partial(rotate_kernel, layers),
        grid=(planes // bx,),
        in_specs=[pl.BlockSpec((grid_count, 2, bx, vy, nz), lambda i: (0, 0, i, 0, 0))] * layers
        + [field_block, field_block],
        out_specs=pl.BlockSpec((layers, 2, bx, ny, nz), lambda i: (0, 0, i, 0, 0)),
        out_shape=jax.ShapeDtypeStruct((layers, 2, planes, ny, nz), jnp.float32),
        compiler_params=pltpu.CompilerParams(vmem_limit_bytes=VMEM_LIMIT),
    )(*returned, cosine, sine)


def table_of(matrix):
    return (np.asarray(matrix.real, np.float32), np.asarray(matrix.imag, np.float32))


def apply_along(values, table, axis):
    contracted = jnp.tensordot(values, table, axes=([axis], [0]), precision=HIGHEST)
    return jnp.moveaxis(contracted, -1, axis)


def complex_along(real_part, imag_part, matrix, axis):
    table_re, table_im = table_of(matrix)
    new_re = apply_along(real_part, table_re, axis) - apply_along(imag_part, table_im, axis)
    new_im = apply_along(real_part, table_im, axis) + apply_along(imag_part, table_re, axis)
    return (new_re, new_im)


def coulomb_kernel(squares_x, squares_y, squares_z):
    total = squares_x[:, None, None] + squares_y[None, :, None] + squares_z[None, None, :]
    anchor = total <= 0.0
    return jnp.where(anchor, 0.0, HARTREE_SCALE / jnp.where(anchor, 1.0, total))


def poisson_shared(density):
    width_x, _, count_z = density.shape
    span_count = lax.axis_size("grid") * lax.axis_size("orb")
    block_x = width_x // span_count
    forward_z = table_of(fourier(count_z, -1))
    real_part, imag_part = (apply_along(density, forward_z[0], 2), apply_along(density, forward_z[1], 2))
    real_part, imag_part = complex_along(real_part, imag_part, fourier(width_x, -1), 0)
    spread = lax.all_to_all(
        jnp.stack([real_part, imag_part], 0),
        ("grid", "orb"),
        split_axis=1,
        concat_axis=2,
        tiled=True,
    )
    count_y = spread.shape[2]
    real_part, imag_part = complex_along(spread[0], spread[1], fourier(count_y, -1), 1)
    start_x = lax.axis_index(("grid", "orb")) * block_x
    squares_x = lax.dynamic_slice_in_dim(
        jnp.asarray(wave_squared(width_x), jnp.float32), start_x, block_x, 0
    )
    kernel = coulomb_kernel(
        squares_x,
        np.asarray(wave_squared(count_y), np.float32),
        np.asarray(wave_squared(count_z), np.float32),
    )
    real_part, imag_part = complex_along(
        real_part * kernel, imag_part * kernel, fourier(count_y, 1) / count_y, 1
    )
    back = lax.all_to_all(
        jnp.stack([real_part, imag_part], 0),
        ("grid", "orb"),
        split_axis=2,
        concat_axis=1,
        tiled=True,
    )
    real_part, imag_part = complex_along(back[0], back[1], fourier(width_x, 1) / width_x, 0)
    inverse_z = table_of(fourier(count_z, 1) / count_z)
    return apply_along(real_part, inverse_z[0], 2) - apply_along(imag_part, inverse_z[1], 2)


def body(orbitals, v_local, occupations):
    layers, _, planes, count_y, count_z = orbitals.shape
    grid_count = lax.axis_size("grid")
    orb_count = lax.axis_size("orb")
    width_x = planes * grid_count
    share_y = count_y // (grid_count * orb_count)
    wz = jnp.asarray(split_const(right_block(kinetic_matrix(count_z))))
    wy = jnp.asarray(split_const(left_block(kinetic_matrix(count_y))))
    order = np.arange(2 * width_x).reshape(2, grid_count, planes).transpose(1, 0, 2).reshape(-1)
    wx = jnp.asarray(split_const(left_block(kinetic_matrix(width_x))[order][:, order]))
    weights = lax.dynamic_slice_in_dim(occupations, lax.axis_index("orb") * layers, layers, 0)
    exchange = partial(lax.all_to_all, axis_name="grid", split_axis=0, concat_axis=0, tiled=True)

    received = [
        exchange(kinetic_local(orbitals, layer, grid_count, wz, wy)) for layer in range(layers)
    ]
    density = None
    returned = []
    for layer in range(layers):
        moved, density = kinetic_across(
            received[layer], weights[layer : layer + 1], density, wx
        )
        returned.append(exchange(moved))
    share = lax.psum_scatter(density, "orb", scatter_dimension=1, tiled=True)
    share, returned[0] = lax.optimization_barrier((share, returned[0]))
    hartree_lines = poisson_shared(share)
    rows_back = lax.all_to_all(hartree_lines, "grid", split_axis=0, concat_axis=1, tiled=True)
    gathered = lax.all_gather(rows_back, "orb", axis=0, tiled=False)
    hartree = gathered.reshape(orb_count, planes, grid_count, share_y, count_z)
    hartree = hartree.transpose(1, 2, 0, 3, 4).reshape(planes, count_y, count_z)
    angle = TIME_STEP * (v_local + hartree)
    return rotate(returned, jnp.cos(angle), jnp.sin(angle))


def solution(mesh):
    return jax.shard_map(
        body,
        mesh=mesh,
        in_specs=(
            P(("groups", "orb"), None, "grid", None, None),
            P(("groups", "grid"), None, None),
            P("groups"),
        ),
        out_specs=P(("groups", "orb"), None, "grid", None, None),
        check_vma=False,
    )
```

profile of v0, /device:TPU:0, one launch (start us, length us, event | category | flops | bytes accessed | tf_op | source)
XLA Modules:
  0.0 566.3 jit_solution(9622674378359005217)
XLA Ops:
  8.4 10.8 %shard_map.272 = f32[4,2,32,32,128]{4,3,2,1,0:T(8,128)} custom-call(f32[4,2,32,128,128]{4,3,2,1,0:T(8,128)} %psi_ref.7, bf16[2,256,256]{2,1,0:T(8,128)(2,1)S(1)} %copy-done.2, bf16[2,256,256]{2,1,0:T(8,128)(2,1)S(1)} %copy-done), custom_call_target="tpu_custom_call" | custom-call | flops 3221225472 | bytes 8388608 | tf_op jit(solution)/shard_map/pallas_call | solution.py:95
  19.3 5.0 all-to-all-start.1
  24.3 10.8 %shard_map.274 = f32[4,2,32,32,128]{4,3,2,1,0:T(8,128)} custom-call(f32[4,2,32,128,128]{4,3,2,1,0:T(8,128)} %psi_ref.7, bf16[2,256,256]{2,1,0:T(8,128)(2,1)S(1)} %copy-done.3, bf16[2,256,256]{2,1,0:T(8,128)(2,1)S(1)} %copy-done.1), custom_call_target="tpu_custom_call" | custom-call | flops 3221225472 | bytes 8388608 | tf_op jit(solution)/shard_map/pallas_call | solution.py:95
  35.2 38.1 %all-to-all-done.1 = f32[4,2,32,32,128]{4,3,2,1,0:T(8,128)} async-done(((f32[4,2,32,32,128]{4,3,2,1,0:T(8,128)}), f32[4,2,32,32,128]{4,3,2,1,0:T(8,128)}, u32[]{:S(2)}, u32[]{:S(2)}) %all-to-all-start.1) | async-done | bytes 4194336 | tf_op jit(solution)/shard_map/all_to_all | solution.py:279
  73.3 4.8 all-to-all-start.3
  78.1 10.9 %shard_map.273 = f32[4,2,32,32,128]{4,3,2,1,0:T(8,128)} custom-call(f32[4,2,32,128,128]{4,3,2,1,0:T(8,128)} %psi_ref.7, bf16[2,256,256]{2,1,0:T(8,128)(2,1)S(1)} %copy-done.3, bf16[2,256,256]{2,1,0:T(8,128)(2,1)S(1)} %copy-done.1), custom_call_target="tpu_custom_call" | custom-call | flops 3221225472 | bytes 8388608 | tf_op jit(solution)/shard_map/pallas_call | solution.py:95
  89.0 37.3 %all-to-all-done.3 = f32[4,2,32,32,128]{4,3,2,1,0:T(8,128)} async-done(((f32[4,2,32,32,128]{4,3,2,1,0:T(8,128)}), f32[4,2,32,32,128]{4,3,2,1,0:T(8,128)}, u32[]{:S(2)}, u32[]{:S(2)}) %all-to-all-start.3) | async-done | bytes 4194336 | tf_op jit(solution)/shard_map/all_to_all | solution.py:279
  126.3 4.9 all-to-all-start.2
  131.2 10.9 %shard_map.271 = f32[4,2,32,32,128]{4,3,2,1,0:T(8,128)} custom-call(f32[4,2,32,128,128]{4,3,2,1,0:T(8,128)} %psi_ref.7, bf16[2,256,256]{2,1,0:T(8,128)(2,1)S(1)} %copy-done.3, bf16[2,256,256]{2,1,0:T(8,128)(2,1)S(1)} %copy-done.1), custom_call_target="tpu_custom_call" | custom-call | flops 3221225472 | bytes 8388608 | tf_op jit(solution)/shard_map/pallas_call | solution.py:95
  142.1 37.3 %all-to-all-done.2 = f32[4,2,32,32,128]{4,3,2,1,0:T(8,128)} async-done(((f32[4,2,32,32,128]{4,3,2,1,0:T(8,128)}), f32[4,2,32,32,128]{4,3,2,1,0:T(8,128)}, u32[]{:S(2)}, u32[]{:S(2)}) %all-to-all-start.2) | async-done | bytes 4194336 | tf_op jit(solution)/shard_map/all_to_all | solution.py:279
  179.4 4.9 all-to-all-start
  185.2 10.2 %shard_map.275 = (f32[256,32,128]{2,1,0:T(8,128)}, f32[128,32,128]{2,1,0:T(8,128)S(1)}) custom-call(f32[1]{0:T(128)} %get-tuple-element.31.weight_ref, f32[256,32,128]{2,1,0:T(8,128)} %bitcast.3.psi_ref, bf16[2,256,256]{2,1,0:T(8,128)(2,1)S(1)} %copy-done.4), custom_call_target="tpu_custom_call" | custom-call | flops 1610612736 | bytes 12582912 | tf_op jit(solution)/shard_map/pallas_call | solution.py:152
  196.8 11.2 %shard_map.276 = (f32[256,32,128]{2,1,0:T(8,128)}, f32[128,32,128]{2,1,0:T(8,128)S(1)}) custom-call(f32[1]{0:T(128)} %get-tuple-element.32.weight_ref, f32[256,32,128]{2,1,0:T(8,128)} %bitcast.2.psi_ref, bf16[2,256,256]{2,1,0:T(8,128)(2,1)S(1)} %copy-done.4, f32[128,32,128]{2,1,0:T(8,128)} %copy-done.7), custom_call_target="tpu_custom_call" | custom-call | flops 1610612736 | bytes 12582912 | tf_op jit(solution)/shard_map/pallas_call | solution.py:152
  209.3 11.3 %shard_map.277 = (f32[256,32,128]{2,1,0:T(8,128)}, f32[128,32,128]{2,1,0:T(8,128)S(1)}) custom-call(f32[1]{0:T(128)} %get-tuple-element.33.weight_ref, f32[256,32,128]{2,1,0:T(8,128)} %bitcast.1.psi_ref, bf16[2,256,256]{2,1,0:T(8,128)(2,1)S(1)} %copy-done.4, f32[128,32,128]{2,1,0:T(8,128)} %copy-done.6), custom_call_target="tpu_custom_call" | custom-call | flops 1610612736 | bytes 12582912 | tf_op jit(solution)/shard_map/pallas_call | solution.py:152
  222.0 10.5 %all-to-all-done = f32[4,2,32,32,128]{4,3,2,1,0:T(8,128)} async-done(((f32[4,2,32,32,128]{4,3,2,1,0:T(8,128)}), f32[4,2,32,32,128]{4,3,2,1,0:T(8,128)}, u32[]{:S(2)}, u32[]{:S(2)}) %all-to-all-start) | async-done | bytes 4194336 | tf_op jit(solution)/shard_map/all_to_all | solution.py:279
  232.5 11.3 %shard_map.278 = (f32[256,32,128]{2,1,0:T(8,128)}, f32[128,32,128]{2,1,0:T(8,128)}) custom-call(f32[1]{0:T(128)} %get-tuple-element.34.weight_ref, f32[256,32,128]{2,1,0:T(8,128)} %bitcast.psi_ref, bf16[2,256,256]{2,1,0:T(8,128)(2,1)S(1)} %copy-done.4, f32[128,32,128]{2,1,0:T(8,128)} %copy-done.5), custom_call_target="tpu_custom_call" | custom-call | flops 1610612736 | bytes 12582912 | tf_op jit(solution)/shard_map/pallas_call | solution.py:152
  243.8 54.0 %all_to_all.85.refs_0_ = f32[4,2,32,32,128]{4,3,2,1,0:T(8,128)} all-to-all(f32[4,2,32,32,128]{4,3,2,1,0:T(8,128)} %bitcast.114), channel_id=1, replica_groups=mesh['groups'=2,'grid'=4,'orb'=4] {'grid'}, dimensions={0} | all-to-all | bytes 8388608 | tf_op jit(solution)/shard_map/all_to_all | solution.py:287
  297.8 1.7 fusion.25
  299.5 1.7 fusion.27
  305.0 5.7 %all-to-all-start.8 = ((f32[2,128,8,128]{3,2,0,1:T(8,128)}), f32[2,128,8,128]{3,2,0,1:T(8,128)S(1)}, u32[]{:S(2)}, u32[]{:S(2)}) async-start(f32[2,128,8,128]{3,2,0,1:T(8,128)} %copy.88), calls=%async_computation.9 | async-start | bytes 2097152 | tf_op jit(solution)/shard_map/all_to_all | solution.py:232
  310.9 26.7 %all-to-all-done.8 = f32[2,128,8,128]{3,2,0,1:T(8,128)S(1)} async-done(((f32[2,128,8,128]{3,2,0,1:T(8,128)}), f32[2,128,8,128]{3,2,0,1:T(8,128)S(1)}, u32[]{:S(2)}, u32[]{:S(2)}) %all-to-all-start.8) | async-done | bytes 1048608 | tf_op jit(solution)/shard_map/all_to_all | solution.py:232
  344.8 30.1 %all_to_all.86 = f32[2,8,128,128]{3,1,0,2:T(8,128)S(1)} all-to-all(f32[2,8,128,128]{3,1,0,2:T(8,128)S(1)} %copy.96), channel_id=1, replica_groups=mesh['groups'=2,'grid'=4,'orb'=4] {'grid','orb'}, dimensions={2} | all-to-all | bytes 2097152 | tf_op jit(solution)/shard_map/all_to_all | solution.py:253
  374.8 5.1 all-to-all-start.5
  385.6 42.3 %all-to-all-done.5.refs_1_ = f32[4,2,32,32,128]{4,3,2,1,0:T(8,128)} async-done(((f32[4,2,32,32,128]{4,3,2,1,0:T(8,128)}), f32[4,2,32,32,128]{4,3,2,1,0:T(8,128)}, u32[]{:S(2)}, u32[]{:S(2)}) %all-to-all-start.5) | async-done | bytes 4194336 | tf_op jit(solution)/shard_map/all_to_all | solution.py:287
  427.9 11.2 %all_to_all.87 = f32[128,8,128]{2,1,0:T(8,128)S(1)} all-to-all(f32[128,8,128]{2,1,0:T(8,128)S(1)} %copy.106), channel_id=1, replica_groups=mesh['groups'=2,'grid'=4,'orb'=4] {'grid'}, dimensions={0} | all-to-all | bytes 1048576 | tf_op jit(solution)/shard_map/all_to_all | solution.py:291
  439.1 4.8 all-to-all-start.6
  444.9 47.3 %all-to-all-done.6.refs_2_ = f32[4,2,32,32,128]{4,3,2,1,0:T(8,128)} async-done(((f32[4,2,32,32,128]{4,3,2,1,0:T(8,128)}), f32[4,2,32,32,128]{4,3,2,1,0:T(8,128)}, u32[]{:S(2)}, u32[]{:S(2)}) %all-to-all-start.6) | async-done | bytes 4194336 | tf_op jit(solution)/shard_map/all_to_all | solution.py:287
  492.1 4.9 all-to-all-start.7
  497.1 2.0 copy.108
  499.3 8.4 %fusion.11 = (f32[32,128,128]{2,1,0:T(8,128)}, f32[32,128,128]{2,1,0:T(8,128)S(1)}) fusion(f32[32,128,128]{2,1,0:T(8,128)S(1)} %copy-done.8, f32[32,4,4,8,128]{4,3,2,1,0:T(8,128)S(1)} %copy.108), kind=kLoop, calls=%fused_computation.24 | loop fusion | flops 1048576 | bytes 8388608 | tf_op jit(solution)/shard_map/sin | solution.py:296
  507.7 37.6 %all-to-all-done.7.refs_3_ = f32[4,2,32,32,128]{4,3,2,1,0:T(8,128)} async-done(((f32[4,2,32,32,128]{4,3,2,1,0:T(8,128)}), f32[4,2,32,32,128]{4,3,2,1,0:T(8,128)}, u32[]{:S(2)}, u32[]{:S(2)}) %all-to-all-start.7) | async-done | bytes 4194336 | tf_op jit(solution)/shard_map/all_to_all | solution.py:287
  545.2 14.3 %shard_map.279 = f32[4,2,32,128,128]{4,3,2,1,0:T(8,128)} custom-call(f32[4,2,32,32,128]{4,3,2,1,0:T(8,128)} %all_to_all.85.refs_0_, f32[4,2,32,32,128]{4,3,2,1,0:T(8,128)} %all-to-all-done.5.refs_1_, f32[4,2,32,32,128]{4,3,2,1,0:T(8,128)} %all-to-all-done.6.refs_2_, f32[4,2,32,32,128]{4,3,2,1,0:T(8,128)} %all-to-all-done.7.refs_3_, ...), custom_call_target="tpu_custom_call" | custom-call | tf_op jit(solution)/shard_map/pallas_call | solution.py:192
  (72 shorter events, 24.6 us)
Async XLA Ops:
  6.5 0.9 copy-start
  7.5 0.9 copy-start.2
  19.3 5.0 copy-start.1
  19.3 5.0 copy-start.3
  19.3 54.0 %all-to-all-start.1 = ((f32[4,2,32,32,128]{4,3,2,1,0:T(8,128)}), f32[4,2,32,32,128]{4,3,2,1,0:T(8,128)}, u32[]{:S(2)}, u32[]{:S(2)}) async-start(f32[4,2,32,32,128]{4,3,2,1,0:T(8,128)} %shard_map.272), calls=%async_computation.1 | async-start | bytes 8388608 | tf_op jit(solution)/shard_map/all_to_all | solution.py:279
  73.3 53.1 %all-to-all-start.3 = ((f32[4,2,32,32,128]{4,3,2,1,0:T(8,128)}), f32[4,2,32,32,128]{4,3,2,1,0:T(8,128)}, u32[]{:S(2)}, u32[]{:S(2)}) async-start(f32[4,2,32,32,128]{4,3,2,1,0:T(8,128)} %shard_map.274), calls=%async_computation.3 | async-start | bytes 8388608 | tf_op jit(solution)/shard_map/all_to_all | solution.py:279
  126.3 53.1 %all-to-all-start.2 = ((f32[4,2,32,32,128]{4,3,2,1,0:T(8,128)}), f32[4,2,32,32,128]{4,3,2,1,0:T(8,128)}, u32[]{:S(2)}, u32[]{:S(2)}) async-start(f32[4,2,32,32,128]{4,3,2,1,0:T(8,128)} %shard_map.273), calls=%async_computation.2 | async-start | bytes 8388608 | tf_op jit(solution)/shard_map/all_to_all | solution.py:279
  142.1 42.4 %copy-start.14 = (f32[16]{0:T(128)S(1)}, f32[16]{0:T(128)}, u32[]{:S(2)}) copy-start(f32[16]{0:T(128)} %param.31) | copy-start | bytes 196
  142.1 43.1 %copy-start.4 = (bf16[2,256,256]{2,1,0:T(8,128)(2,1)S(1)}, bf16[2,256,256]{2,1,0:T(8,128)(2,1)}, u32[]{:S(2)}) copy-start(bf16[2,256,256]{2,1,0:T(8,128)(2,1)} %constant.48.clone.wx_ref) | copy-start | bytes 786436
  179.4 53.1 %all-to-all-start = ((f32[4,2,32,32,128]{4,3,2,1,0:T(8,128)}), f32[4,2,32,32,128]{4,3,2,1,0:T(8,128)}, u32[]{:S(2)}, u32[]{:S(2)}) async-start(f32[4,2,32,32,128]{4,3,2,1,0:T(8,128)} %shard_map.271), calls=%async_computation | async-start | bytes 8388608 | tf_op jit(solution)/shard_map/all_to_all | solution.py:279
  184.3 113.5 %reduce-scatter.2.cloned.1.call-start = ((), (), s32[]{:S(2)}) async-start(), calls=%async_computation.12 | async-start | bytes 2621440 | tf_op jit(solution)/shard_map/reduce_scatter | solution.py:288
  195.4 1.4 copy-start.7
  208.0 1.4 copy-start.6
  220.6 1.4 copy-start.5
  243.8 54.0 %copy-start.11 = (f32[128,128,1]{1,0,2:T(8,128)S(1)}, f32[128,128,1]{1,0,2:T(8,128)}, u32[]{:S(2)}) copy-start(f32[128,128,1]{1,0,2:T(8,128)} %constant.60) | copy-start | bytes 196612
  243.8 55.7 %copy-start.12 = (f32[128,128,1]{1,0,2:T(8,128)S(1)}, f32[128,128,1]{1,0,2:T(8,128)}, u32[]{:S(2)}) copy-start(f32[128,128,1]{1,0,2:T(8,128)} %constant.59) | copy-start | bytes 196612
  302.9 7.8 %copy-start.13 = (f32[128]{0:T(128)S(1)}, f32[128]{0:T(128)}, u32[]{:S(2)}) copy-start(f32[128]{0:T(128)} %constant.51.clone) | copy-start | bytes 1540
  305.0 32.5 %all-to-all-start.8 = ((f32[2,128,8,128]{3,2,0,1:T(8,128)}), f32[2,128,8,128]{3,2,0,1:T(8,128)S(1)}, u32[]{:S(2)}, u32[]{:S(2)}) async-start(f32[2,128,8,128]{3,2,0,1:T(8,128)} %copy.88), calls=%async_computation.9 | async-start | bytes 2097152 | tf_op jit(solution)/shard_map/all_to_all | solution.py:232
  337.7 4.2 copy-start.9
  338.7 3.8 copy-start.10
  374.8 53.1 %all-to-all-start.5 = ((f32[4,2,32,32,128]{4,3,2,1,0:T(8,128)}), f32[4,2,32,32,128]{4,3,2,1,0:T(8,128)}, u32[]{:S(2)}, u32[]{:S(2)}) async-start(f32[4,2,32,32,128]{4,3,2,1,0:T(8,128)} %bitcast.113), calls=%async_computation.6 | async-start | bytes 8388608 | tf_op jit(solution)/shard_map/all_to_all | solution.py:287
  439.1 53.1 %all-to-all-start.6 = ((f32[4,2,32,32,128]{4,3,2,1,0:T(8,128)}), f32[4,2,32,32,128]{4,3,2,1,0:T(8,128)}, u32[]{:S(2)}, u32[]{:S(2)}) async-start(f32[4,2,32,32,128]{4,3,2,1,0:T(8,128)} %bitcast.112), calls=%async_computation.7 | async-start | bytes 8388608 | tf_op jit(solution)/shard_map/all_to_all | solution.py:287
  443.9 53.1 %all-gather.2.cloned.1.call-start = ((), (), s32[]{:S(2)}) async-start(), calls=%async_computation.13 | async-start | bytes 2621440 | tf_op jit(solution)/shard_map/all_gather | solution.py:292
  492.1 53.1 %all-to-all-start.7 = ((f32[4,2,32,32,128]{4,3,2,1,0:T(8,128)}), f32[4,2,32,32,128]{4,3,2,1,0:T(8,128)}, u32[]{:S(2)}, u32[]{:S(2)}) async-start(f32[4,2,32,32,128]{4,3,2,1,0:T(8,128)} %bitcast.111), calls=%async_computation.8 | async-start | bytes 8388608 | tf_op jit(solution)/shard_map/all_to_all | solution.py:287
  497.0 2.2 copy-start.8
Sparse Core Ops, SparseCore 0:
  243.9 44.6 reduce-scatter.1
  446.3 44.6 all-gather.1
where the time goes:
time: 568 us; the launch traced here: 566 us
  waiting for transfers between devices  277 us (49%)
  Pallas kernels  102 us (18%)
  blocking collectives  95.2 us (17%)
  starting transfers between devices  40.4 us (7%)
  matrix products  16.3 us (3%)
  between operations  13.9 us (2%)
  local copies, waits for them, and re-layouts  13.2 us (2%)
  other arithmetic  8.6 us (2%)
    all_to_all x3, waiting for transfers between devices, body(): returned.append(exchange(moved))  127 us
    all_to_all x4, waiting for transfers between devices, body(): exchange(kinetic_local(orbitals, layer, grid_count, wz, wy))  123 us
    all_to_all x1, blocking collectives, body(): returned.append(exchange(moved))  54 us
    pallas_call x4, Pallas kernels, kinetic_across(): pl.pallas_call(partial(across_kernel, planes, first), grid=(vy // by,), i...  43.9 us
    pallas_call x4, Pallas kernels, kinetic_local(): pl.pallas_call(local_kernel, grid=(planes // bx,), in_specs=[pl.BlockSpec...  43.4 us
    all_to_all x1, blocking collectives, poisson_shared(): lax.all_to_all(jnp.stack([real_part, imag_part], 0), ('grid', 'orb'), spl...  30.1 us
    all_to_all x1, waiting for transfers between devices, poisson_shared(): lax.all_to_all(jnp.stack([real_part, imag_part], 0), ('grid', 'orb'), spl...  26.7 us
    all_to_all x4, starting transfers between devices, body(): exchange(kinetic_local(orbitals, layer, grid_count, wz, wy))  19.6 us
  transfers between devices with their start and end apart: 10, of which 8 were waited for; matrix products, arithmetic and copies ran while one was open for 3% of the time, Pallas kernels for 12%

commit v1 on v0

--- a/solution.py
+++ b/solution.py
@@ -168,6 +168,380 @@
     return moved.reshape(grid_count, 2, planes, vy, nz), density
 
 
+LANE_ROWS = 8
+MESH = pl.DeviceIdType.MESH
+EPS = float(np.finfo(np.float32).eps)
+
+
+def far_factors(block):
+    block = block.astype(np.clongdouble)
+    norm2 = np.sum(np.abs(block) ** 2)
+    residual = block.copy()
+    rank = 0
+    basis = []
+    for _ in range(block.shape[1]):
+        sizes = np.sum(np.abs(residual) ** 2, axis=1)
+        if np.sum(sizes) <= (EPS * EPS) * 1e-3 * norm2:
+            break
+        row = residual[int(np.argmax(sizes))].conj()
+        for other in basis:
+            row = row - other * np.sum(other.conj() * row)
+        row = row / np.sqrt(np.sum(np.abs(row) ** 2))
+        basis.append(row)
+        residual = residual - np.sum(residual * row[None, :], axis=1)[:, None] * row.conj()[None, :]
+    gram = np.matmul(block.conj().T, block)
+    for _ in range(8):
+        basis = [np.sum(gram * vector[None, :], axis=1) for vector in basis]
+        clean = []
+        for row in basis:
+            for _ in range(2):
+                for other in clean:
+                    row = row - other * np.sum(other.conj() * row)
+            clean.append(row / np.sqrt(np.sum(np.abs(row) ** 2)))
+        basis = clean
+    for rank in range(1, len(basis) + 1):
+        right = np.stack(basis[:rank], 1)
+        left = np.matmul(block, right)
+        rest = block - np.matmul(left, right.conj().T)
+        if np.linalg.norm(rest.astype(np.complex128), 2) <= EPS:
+            break
+    return left.astype(np.complex128), right.astype(np.complex128)
+
+
+def real_form(matrix):
+    return np.block([[matrix.real, -matrix.imag], [matrix.imag, matrix.real]])
+
+
+def stacked_table(table):
+    high, low = split_const(table).astype(np.float32)
+    return np.block([[high, high], [low, np.zeros_like(low)]]).astype(ml_dtypes.bfloat16)
+
+
+def evolve_tables(width_x, planes):
+    matrix = kinetic_matrix(width_x)
+    half = 2 * planes
+    left, right = far_factors(matrix[half:, :half])
+    rank = -(-left.shape[1] // 2) * 2
+    pad = rank - left.shape[1]
+    left = np.pad(left, ((0, 0), (0, pad)))
+    right = np.pad(right, ((0, 0), (0, pad)))
+    near = matrix[:planes, :planes]
+    sides = []
+    for core in range(2):
+        mine = slice(core * planes, (core + 1) * planes)
+        theirs = slice((1 - core) * planes, (2 - core) * planes)
+        sides.append(
+            (left[mine], right[mine], far_factors(matrix[theirs, mine]), far_factors(matrix[mine, theirs]))
+        )
+    core_rank = max(s[2][0].shape[1] for s in sides)
+    core_rank = -(-core_rank // 4) * 4
+    widen = lambda m: np.pad(m, ((0, 0), (0, core_rank - m.shape[1])))
+    far = -(-2 * rank // 8) * 8
+    gather, spread = [], []
+    for mine_left, mine_right, (_, give), (take, _) in sides:
+        rows = real_form(mine_right.conj().T)
+        rows = np.concatenate([rows, np.zeros((far - rows.shape[0], rows.shape[1]))], 0)
+        core_rows = real_form(widen(give).conj().T)
+        gather.append(stacked_table(np.concatenate([rows, core_rows], 0)))
+        far_columns = real_form(mine_left)
+        far_columns = np.pad(far_columns, ((0, 0), (0, far - far_columns.shape[1])))
+        spread.append(
+            stacked_table(np.concatenate([real_form(near), real_form(widen(take)), far_columns], 1))
+        )
+    return np.stack(gather), np.stack(spread), 2 * rank, far, 2 * core_rank
+
+
+def stack_split(values):
+    high, low = split(values)
+    return jnp.concatenate([high, low], 0)
+
+
+def evolve_kernel(
+    layers, far_rows, far, near_rows, lag,
+    weight_ref, psi_ref, wz_ref, wy_ref, gather_ref, spread_ref,
+    out_ref, density_ref,
+    stage, phi, give_far, give_near, got_far, got_near, far_field, result, density,
+    in_sem, out_sem, p_send, p_recv, q_send, q_recv, y_send, y_recv, f_send, f_recv, density_sem,
+):
+    _, _, planes, ny, nz = psi_ref.shape
+    groups = ny // LANE_ROWS
+    tiles = groups // 2
+    units = layers * tiles
+    bx = planes // tiles
+    place = lax.axis_index("grid")
+    core = lax.rem(place, 2)
+    sibling = place + 1 - 2 * core
+    across = lax.rem(place + 2, 4)
+
+    def far_copy(unit):
+        return pltpu.make_async_remote_copy(
+            src_ref=give_far.at[lax.rem(unit, 4), 1 - core], dst_ref=got_far.at[unit],
+            send_sem=p_send.at[unit], recv_sem=p_recv.at[unit],
+            device_id={"grid": sibling}, device_id_type=MESH,
+        )
+
+    def near_copy(unit):
+        return pltpu.make_async_remote_copy(
+            src_ref=give_near.at[lax.rem(unit, 4)], dst_ref=got_near.at[unit],
+            send_sem=q_send.at[unit], recv_sem=q_recv.at[unit],
+            device_id={"grid": sibling}, device_id_type=MESH,
+        )
+
+    def across_copy(unit):
+        return pltpu.make_async_remote_copy(
+            src_ref=got_far.at[unit], dst_ref=far_field.at[unit, core, pl.ds(0, far_rows)],
+            send_sem=y_send.at[unit], recv_sem=y_recv.at[unit],
+            device_id={"grid": across}, device_id_type=MESH,
+        )
+
+    def share_copy(unit):
+        held = far_field.at[unit, core, pl.ds(0, far_rows)]
+        return pltpu.make_async_remote_copy(
+            src_ref=held, dst_ref=held,
+            send_sem=f_send.at[unit], recv_sem=f_recv.at[unit],
+            device_id={"grid": sibling}, device_id_type=MESH,
+        )
+
+    def load_copy(step):
+        layer, part = step // tiles, lax.rem(step, tiles)
+        slot = lax.rem(step, 3)
+        return pltpu.make_async_copy(
+            psi_ref.at[layer, :, pl.ds(part * bx, bx)], stage.at[slot], in_sem.at[slot]
+        )
+
+    def result_copy(unit, half):
+        layer, tile = unit // tiles, lax.rem(unit, tiles)
+        slot = lax.rem(unit, 3)
+        row = pl.multiple_of((2 * tile + half) * LANE_ROWS, LANE_ROWS)
+        return pltpu.make_async_copy(
+            result.at[slot, half],
+            out_ref.at[layer, :, pl.ds(row, LANE_ROWS), :],
+            out_sem.at[slot, half],
+        )
+
+    load_copy(0).start()
+    load_copy(1).start()
+    if far > far_rows:
+        far_field[:, :, far_rows:] = jnp.zeros((units, 2, far - far_rows, LANE_ROWS, nz), jnp.float32)
+    barrier = pltpu.get_barrier_semaphore()
+    for peer in (sibling, across):
+        pl.semaphore_signal(barrier, inc=1, device_id={"grid": peer}, device_id_type=MESH)
+    pl.semaphore_wait(barrier, 2)
+
+    def plane_step(step):
+        @pl.when(step + 2 < units)
+        def _():
+            load_copy(step + 2).start()
+
+        load_copy(step).wait()
+        layer, part = step // tiles, lax.rem(step, tiles)
+        slot = lax.rem(step, 3)
+        real_part = stage[slot, 0].reshape(bx * ny, nz)
+        imag_part = stage[slot, 1].reshape(bx * ny, nz)
+        turned = data_by_table(jnp.concatenate([real_part, imag_part], 1), wz_ref)
+        columns = [
+            jnp.concatenate([turned[p * ny : (p + 1) * ny, :nz], turned[p * ny : (p + 1) * ny, nz:]], 0)
+            for p in range(bx)
+        ]
+        rows = table_by_data(wy_ref, jnp.concatenate(columns, 1))
+        for c in range(2):
+            for p in range(bx):
+                block = rows[c * ny : (c + 1) * ny, p * nz : (p + 1) * nz]
+                phi[layer, :, c * planes + part * bx + p] = block.reshape(groups, LANE_ROWS, nz)
+
+    def gather_step(unit):
+        layer, tile = unit // tiles, lax.rem(unit, tiles)
+        slot = lax.rem(unit, 4)
+
+        @pl.when(unit >= 4)
+        def _():
+            far_copy(unit - 4).wait_send()
+            near_copy(unit - 4).wait_send()
+
+        for half in range(2):
+            for part in range(2):
+                ids = range(4 * part, 4 * part + 4)
+                data = jnp.concatenate([phi[layer, 2 * tile + half, :, i, :] for i in ids], 1)
+                both = dot(gather_ref[core], stack_split(data))
+                total = both[: far + near_rows] + both[far + near_rows :]
+                for k, i in enumerate(ids):
+                    block = total[:, k * nz : (k + 1) * nz]
+                    give_far[slot, half, :, i, :] = block[:far_rows]
+                    give_near[slot, half, :, i, :] = block[far:]
+
+    def sum_step(unit):
+        far_copy(unit).wait_recv()
+        got_far[unit] = got_far[unit] + give_far[lax.rem(unit, 4), core]
+
+    def spread_step(unit):
+        layer, tile = unit // tiles, lax.rem(unit, tiles)
+        slot = lax.rem(unit, 3)
+        near_copy(unit).wait_recv()
+        share_copy(unit).wait_recv()
+
+        @pl.when(unit >= 3)
+        def _():
+            result_copy(unit - 3, 0).wait()
+            result_copy(unit - 3, 1).wait()
+
+        weight = weight_ref[layer]
+        for half in range(2):
+            for part in range(2):
+                ids = range(4 * part, 4 * part + 4)
+                data = jnp.concatenate(
+                    [
+                        jnp.concatenate(
+                            [
+                                phi[layer, 2 * tile + half, :, i, :],
+                                got_near[unit, half, :, i, :],
+                                far_field[unit, half, :, i, :],
+                            ],
+                            0,
+                        )
+                        for i in ids
+                    ],
+                    1,
+                )
+                both = dot(spread_ref[core], stack_split(data))
+                moved = both[: 2 * planes] + both[2 * planes :]
+                squares = moved * moved
+                term = weight * (squares[:planes] + squares[planes:])
+                for k, i in enumerate(ids):
+                    result[slot, half, :, i, :] = moved[:, k * nz : (k + 1) * nz]
+                    earlier = density[2 * tile + half, :, i, :]
+                    value = term[:, k * nz : (k + 1) * nz]
+                    density[2 * tile + half, :, i, :] = value + jnp.where(layer == 0, 0.0, earlier)
+
+    first_gather = tiles
+    first_forward = tiles + 3 + lag
+    first_spread = first_forward + 2
+
+    def tick(t, carry):
+        def stage_at(start, action):
+            unit = t - start
+
+            @pl.when((unit >= 0) & (unit < units))
+            def _():
+                action(unit)
+
+        def send(unit):
+            far_copy(unit).start()
+            near_copy(unit).start()
+
+        def forward(unit):
+            across_copy(unit).wait_recv()
+            share_copy(unit).start()
+
+        def write(unit):
+            result_copy(unit, 0).start()
+            result_copy(unit, 1).start()
+
+        stage_at(first_gather + 1, send)
+        stage_at(first_gather + 3, lambda unit: across_copy(unit).start())
+        stage_at(first_spread + 1, write)
+        stage_at(0, plane_step)
+        stage_at(first_gather + 2, sum_step)
+        stage_at(first_gather, gather_step)
+        stage_at(first_forward, forward)
+        stage_at(first_spread, spread_step)
+        return carry
+
+    density[...] = jnp.zeros_like(density)
+    lax.fori_loop(0, first_spread + 1 + units, tick, 0)
+
+    for g in range(groups):
+        pltpu.make_async_copy(
+            density.at[g], density_ref.at[:, pl.ds(g * LANE_ROWS, LANE_ROWS), :], density_sem.at[g]
+        ).start()
+
+    def finish(unit, carry):
+        across_copy(unit).wait_send()
+        share_copy(unit).wait_send()
+
+        @pl.when(unit >= units - 4)
+        def _():
+            far_copy(unit).wait_send()
+            near_copy(unit).wait_send()
+
+        @pl.when(unit >= units - 3)
+        def _():
+            result_copy(unit, 0).wait()
+            result_copy(unit, 1).wait()
+
+        return carry
+
+    lax.fori_loop(0, units, finish, 0)
+    for g in range(groups):
+        pltpu.make_async_copy(
+            density.at[g], density_ref.at[:, pl.ds(g * LANE_ROWS, LANE_ROWS), :], density_sem.at[g]
+        ).wait()
+
+
+def evolve(orbitals, weights, wz, wy):
+    layers, _, planes, ny, nz = orbitals.shape
+    gather, spread, far_rows, far, near_rows = evolve_tables(4 * planes, planes)
+    groups = ny // LANE_ROWS
+    units = layers * groups // 2
+    f32 = jnp.float32
+    vmem = pl.BlockSpec(memory_space=pltpu.VMEM)
+    anywhere = pl.BlockSpec(memory_space=pl.ANY)
+    dma = pltpu.SemaphoreType.DMA
+    evolved, density = pl.pallas_call(
+        partial(evolve_kernel, layers, far_rows, far, near_rows, 3),
+        in_specs=[pl.BlockSpec(memory_space=pltpu.SMEM), anywhere, vmem, vmem, vmem, vmem],
+        out_specs=[anywhere, anywhere],
+        out_shape=[
+            jax.ShapeDtypeStruct((layers, 2 * planes, ny, nz), f32),
+            jax.ShapeDtypeStruct((planes, ny, nz), f32),
+        ],
+        scratch_shapes=[
+            pltpu.VMEM((3, 2, planes * 2 // groups, ny, nz), f32),
+            pltpu.VMEM((layers, groups, 2 * planes, LANE_ROWS, nz), f32),
+            pltpu.VMEM((4, 2, far_rows, LANE_ROWS, nz), f32),
+            pltpu.VMEM((4, 2, near_rows, LANE_ROWS, nz), f32),
+            pltpu.VMEM((units, far_rows, LANE_ROWS, nz), f32),
+            pltpu.VMEM((units, 2, near_rows, LANE_ROWS, nz), f32),
+            pltpu.VMEM((units, 2, far, LANE_ROWS, nz), f32),
+            pltpu.VMEM((3, 2, 2 * planes, LANE_ROWS, nz), f32),
+            pltpu.VMEM((groups, planes, LANE_ROWS, nz), f32),
+            dma((3,)),
+            dma((3, 2)),
+        ]
+        + [dma((units,))] * 8
+        + [dma((groups,))],
+        compiler_params=pltpu.CompilerParams(
+            vmem_limit_bytes=60 * 1024 * 1024, collective_id=0, has_side_effects=True
+        ),
+        cost_estimate=pl.CostEstimate(
+            flops=40 * layers * planes * ny * nz * (ny + nz), bytes_accessed=16 * layers * planes * ny * nz, transcendentals=0
+        ),
+    )(weights, orbitals, wz, wy, jnp.asarray(gather), jnp.asarray(spread))
+    return evolved.reshape(layers, 2, planes, ny, nz), density
+
+
+def turn_kernel(psi_ref, cos_ref, sin_ref, out_ref):
+    cosine, sine = cos_ref[...], sin_ref[...]
+    for l in range(psi_ref.shape[0]):
+        real_part, imag_part = psi_ref[l, 0], psi_ref[l, 1]
+        out_ref[l, 0] = real_part * cosine + imag_part * sine
+        out_ref[l, 1] = imag_part * cosine - real_part * sine
+
+
+def turn(evolved, cosine, sine):
+    layers, _, planes, ny, nz = evolved.shape
+    bx = min(4, planes)
+    field_block = pl.BlockSpec((bx, ny, nz), lambda i: (i, 0, 0))
+    block = pl.BlockSpec((layers, 2, bx, ny, nz), lambda i: (0, 0, i, 0, 0))
+    return pl.pallas_call(
+        turn_kernel,
+        grid=(planes // bx,),
+        in_specs=[block, field_block, field_block],
+        out_specs=block,
+        out_shape=jax.ShapeDtypeStruct(evolved.shape, jnp.float32),
+        compiler_params=pltpu.CompilerParams(vmem_limit_bytes=VMEM_LIMIT),
+    )(evolved, cosine, sine)
+
+
 def rotate_kernel(layers, *refs):
     cos_ref, sin_ref = refs[layers], refs[layers + 1]
     out_ref = refs[layers + 2]
@@ -222,7 +596,7 @@
     return jnp.where(anchor, 0.0, HARTREE_SCALE / jnp.where(anchor, 1.0, total))
 
 
-def poisson_shared(density):
+def poisson_shared(density, names):
     width_x, _, count_z = density.shape
     span_count = lax.axis_size("grid") * lax.axis_size("orb")
     block_x = width_x // span_count
@@ -231,14 +605,14 @@
     real_part, imag_part = complex_along(real_part, imag_part, fourier(width_x, -1), 0)
     spread = lax.all_to_all(
         jnp.stack([real_part, imag_part], 0),
-        ("grid", "orb"),
+        names,
         split_axis=1,
         concat_axis=2,
         tiled=True,
     )
     count_y = spread.shape[2]
     real_part, imag_part = complex_along(spread[0], spread[1], fourier(count_y, -1), 1)
-    start_x = lax.axis_index(("grid", "orb")) * block_x
+    start_x = lax.axis_index(names) * block_x
     squares_x = lax.dynamic_slice_in_dim(
         jnp.asarray(wave_squared(width_x), jnp.float32), start_x, block_x, 0
     )
@@ -252,7 +626,7 @@
     )
     back = lax.all_to_all(
         jnp.stack([real_part, imag_part], 0),
-        ("grid", "orb"),
+        names,
         split_axis=2,
         concat_axis=1,
         tiled=True,
@@ -273,6 +647,15 @@
     order = np.arange(2 * width_x).reshape(2, grid_count, planes).transpose(1, 0, 2).reshape(-1)
     wx = jnp.asarray(split_const(left_block(kinetic_matrix(width_x))[order][:, order]))
     weights = lax.dynamic_slice_in_dim(occupations, lax.axis_index("orb") * layers, layers, 0)
+    if grid_count == 4 and 2 * planes % (count_y // LANE_ROWS) == 0 and count_y % (2 * LANE_ROWS) == 0:
+        evolved, density = evolve(orbitals, weights, wz, wy)
+        share = lax.psum_scatter(density, "orb", scatter_dimension=1, tiled=True)
+        lines = lax.all_to_all(share, "grid", split_axis=1, concat_axis=0, tiled=True)
+        hartree_lines = poisson_shared(lines, ("orb", "grid"))
+        rows_back = lax.all_to_all(hartree_lines, "grid", split_axis=0, concat_axis=1, tiled=True)
+        hartree = lax.all_gather(rows_back, "orb", axis=1, tiled=True)
+        angle = TIME_STEP * (v_local + hartree)
+        return turn(evolved, jnp.cos(angle), jnp.sin(angle))
     exchange = partial(lax.all_to_all, axis_name="grid", split_axis=0, concat_axis=0, tiled=True)
 
     received = [
@@ -287,7 +670,7 @@
         returned.append(exchange(moved))
     share = lax.psum_scatter(density, "orb", scatter_dimension=1, tiled=True)
     share, returned[0] = lax.optimization_barrier((share, returned[0]))
-    hartree_lines = poisson_shared(share)
+    hartree_lines = poisson_shared(share, ("grid", "orb"))
     rows_back = lax.all_to_all(hartree_lines, "grid", split_axis=0, concat_axis=1, tiled=True)
     gathered = lax.all_gather(rows_back, "orb", axis=0, tiled=False)
     hartree = gathered.reshape(orb_count, planes, grid_count, share_y, count_z)

time: 568 us -> 341 us (0.60)
  waiting for transfers between devices: 277 us -> 112 us
  blocking collectives: 95.2 us -> 54.4 us
  starting transfers between devices: 40.4 us -> 3.88 us
  Pallas kernels: 102 us -> 125 us
  local copies, waits for them, and re-layouts: 13.2 us -> 6.92 us
    all_to_all x8 -> x1, waiting for transfers between devices: 277 us -> 22.5 us  [poisson_shared(): lax.all_to_all(jnp.stack([real_part, imag_part], 0), names, split_axis=1,...]
    all_gather x1, waiting for transfers between devices: 0.02 us -> 45.2 us  [body(): hartree = lax.all_gather(rows_back, 'orb', axis=1, tiled=True)]
    reduce_scatter x1, waiting for transfers between devices: 0.01 us -> 44.5 us  [body(): share = lax.psum_scatter(density, 'orb', scatter_dimension=1, tiled=True)]
    all_to_all x2, blocking collectives: 84 us -> 42.6 us  [the longest x1 31.2 us: poisson_shared(): lax.all_to_all(jnp.stack([real_part, imag_part], 0), names, split_axis=2,...]
    all_to_all x8 -> x1, starting transfers between devices: 40.1 us -> 3.66 us  [poisson_shared(): lax.all_to_all(jnp.stack([real_part, imag_part], 0), names, split_axis=1,...]
    pallas_call x9 -> x2, Pallas kernels: 102 us -> 125 us  [the longest x1 110 us: evolve(): pl.pallas_call(partial(evolve_kernel, layers, far_rows, far, near_rows, 3...]
    unnamed x30 -> x12, local copies, waits for them, and re-layouts: 6.25 us -> 0.04 us
  transfers between devices with their start and end apart: 10 -> 3, of which waited for: 8 -> 3; matrix products, arithmetic and copies ran while one was open for 3% -> 0% of each run, Pallas kernels for 12% -> 0%
where the time goes in v1:
time: 341 us; the launch traced here: 340 us
  Pallas kernels  125 us (37%)
  waiting for transfers between devices  112 us (33%)
  blocking collectives  54.4 us (16%)
  matrix products  14.1 us (4%)
  between operations  13.8 us (4%)
  other arithmetic  9.74 us (3%)
  local copies, waits for them, and re-layouts  6.92 us (2%)
  starting transfers between devices  3.88 us (1%)
    pallas_call x1, Pallas kernels, evolve(): pl.pallas_call(partial(evolve_kernel, layers, far_rows, far, near_rows, 3...  110 us
    all_gather x1, waiting for transfers between devices, body(): hartree = lax.all_gather(rows_back, 'orb', axis=1, tiled=True)  45.2 us
    reduce_scatter x1, waiting for transfers between devices, body(): share = lax.psum_scatter(density, 'orb', scatter_dimension=1, tiled=True)  44.5 us
    all_to_all x1, blocking collectives, poisson_shared(): lax.all_to_all(jnp.stack([real_part, imag_part], 0), names, split_axis=2,...  31.2 us
    all_to_all x1, waiting for transfers between devices, poisson_shared(): lax.all_to_all(jnp.stack([real_part, imag_part], 0), names, split_axis=1,...  22.5 us
    pallas_call x1, Pallas kernels, turn(): pl.pallas_call(turn_kernel, grid=(planes // bx,), in_specs=[block, field_...  14.8 us
    dot_general x20, matrix products, apply_along(): jnp.tensordot(values, table, axes=([axis], [0]), precision=HIGHEST)  14.1 us
    all_to_all x1, blocking collectives, body(): lax.all_to_all(hartree_lines, 'grid', split_axis=0, concat_axis=1, tiled=...  11.9 us
  transfers between devices with their start and end apart: 3, of which 3 were waited for; matrix products, arithmetic and copies ran while one was open for 0% of the time, Pallas kernels for 0%

profile of v1, /device:TPU:0, one launch (start us, length us, event | category | flops | bytes accessed | tf_op | source)
XLA Modules:
  0.0 340.1 jit_solution(1202366297875938249)
XLA Ops:
  6.5 1.2 dynamic_slice.6.weight_ref
  7.8 110.3 %shard_map.280 = (f32[4,64,128,128]{3,2,1,0:T(8,128)}, f32[32,128,128]{2,1,0:T(8,128)}) custom-call(f32[4]{0:T(128)} %dynamic_slice.6.weight_ref, f32[4,2,32,128,128]{4,3,2,1,0:T(8,128)} %psi_ref.1, bf16[2,256,256]{2,1,0:T(8,128)(2,1)} %constant.48.clone.wz_ref, bf16[2,256,256]{2,1,0:T(8,128)(2,1)} %constant.49.clone.wy_ref, ...), custom_call_target="tpu_custom_call" | custom-call | flops 21474836480 | bytes 33554432 | tf_op jit(solution)/shard_map/pallas_call | solution.py:489
  118.2 44.5 %reduce-scatter.2.cloned.1.call-done = f32[32,32,128]{2,1,0:T(8,128)} async-done(((f32[32,128,128]{2,1,0:T(8,128)}), f32[32,32,128]{2,1,0:T(8,128)}) %reduce-scatter.2.cloned.1.call-update) | async-done | bytes 524304 | tf_op jit(solution)/shard_map/reduce_scatter | solution.py:652
  162.6 1.3 copy.55
  164.0 11.3 %all_to_all.66 = f32[32,32,128]{2,0,1:T(8,128)S(1)} all-to-all(f32[32,32,128]{2,0,1:T(8,128)S(1)} %copy.55), channel_id=1, replica_groups=mesh['groups'=2,'grid'=4,'orb'=4] {'grid'}, dimensions={1} | all-to-all | bytes 1048576 | tf_op jit(solution)/shard_map/all_to_all | solution.py:653
  175.4 0.6 fusion.28
  176.0 0.6 fusion.26
  176.6 0.6 fusion.27
  177.8 0.6 fusion.8
  178.4 0.6 fusion.9
  179.0 1.4 copy.61
  180.4 3.7 %all-to-all-start.1 = ((f32[2,128,8,128]{3,2,0,1:T(8,128)}), f32[2,128,8,128]{3,2,0,1:T(8,128)S(1)}, u32[]{:S(2)}, u32[]{:S(2)}) async-start(f32[2,128,8,128]{3,2,0,1:T(8,128)} %copy.61), calls=%async_computation.2 | async-start | bytes 2097152 | tf_op jit(solution)/shard_map/all_to_all | solution.py:606
  184.5 22.5 %all-to-all-done.1 = f32[2,128,8,128]{3,2,0,1:T(8,128)S(1)} async-done(((f32[2,128,8,128]{3,2,0,1:T(8,128)}), f32[2,128,8,128]{3,2,0,1:T(8,128)S(1)}, u32[]{:S(2)}, u32[]{:S(2)}) %all-to-all-start.1) | async-done | bytes 1048608 | tf_op jit(solution)/shard_map/all_to_all | solution.py:606
  207.1 1.0 fusion.16
  208.1 1.0 fusion.18
  209.1 1.1 fusion.5
  210.2 1.1 fusion.7
  211.9 0.6 fusion.30
  212.4 0.6 fusion.3
  213.0 0.6 fusion.2
  214.2 31.2 %all_to_all.67 = f32[2,8,128,128]{3,1,0,2:T(8,128)S(1)} all-to-all(f32[2,8,128,128]{3,1,0,2:T(8,128)S(1)} %copy.69), channel_id=1, replica_groups=mesh['groups'=2,'grid'=4,'orb'=4] {'orb','grid'}, dimensions={2} | all-to-all | bytes 2097152 | tf_op jit(solution)/shard_map/all_to_all | solution.py:627
  246.1 0.6 fusion.34
  246.7 0.6 fusion.32
  247.6 0.6 fusion.1
  248.1 0.6 fusion
  248.7 1.0 fusion.33
  249.7 1.0 convolution_subtract_fusion
  251.0 11.9 %all_to_all.68 = f32[128,8,128]{2,1,0:T(8,128)S(1)} all-to-all(f32[128,8,128]{2,1,0:T(8,128)S(1)} %copy.79), channel_id=1, replica_groups=mesh['groups'=2,'grid'=4,'orb'=4] {'grid'}, dimensions={0} | all-to-all | bytes 1048576 | tf_op jit(solution)/shard_map/all_to_all | solution.py:655
  262.9 0.9 copy.108
  263.8 45.2 %all-gather.2.cloned.1.call-done = f32[32,128,128]{2,1,0:T(8,128)} async-done(((f32[32,32,128]{2,1,0:T(8,128)}), f32[32,128,128]{2,1,0:T(8,128)}) %all-gather.2.cloned.1.call-update) | async-done | bytes 2097168 | tf_op jit(solution)/shard_map/all_gather | solution.py:656
  309.0 9.5 %fusion.10 = (f32[32,128,128]{2,1,0:T(8,128)}, f32[32,128,128]{2,1,0:T(8,128)S(1)}) fusion(f32[32,128,128]{2,1,0:T(8,128)S(1)} %copy-done, f32[32,128,128]{2,1,0:T(8,128)} %all-gather.2.cloned.1.call-done), kind=kLoop, calls=%fused_computation.23 | loop fusion | flops 1048576 | bytes 8388608 | tf_op jit(solution)/shard_map/sin | solution.py:658
  318.5 14.8 %shard_map.281 = f32[4,2,32,128,128]{4,3,2,1,0:T(8,128)} custom-call(f32[4,2,32,128,128]{4,3,2,1,0:T(8,128)} %bitcast.99, f32[32,128,128]{2,1,0:T(8,128)S(1)} %get-tuple-element.10.cos_ref, f32[32,128,128]{2,1,0:T(8,128)} %get-tuple-element.9.sin_ref), custom_call_target="tpu_custom_call" | custom-call | tf_op jit(solution)/shard_map/pallas_call | solution.py:535
  (33 shorter events, 3.7 us)
Async XLA Ops:
  6.5 156.1 %reduce-scatter.2.cloned.1.call-start = ((), (), s32[]{:S(2)}) async-start(), calls=%async_computation.5 | async-start | bytes 2621440 | tf_op jit(solution)/shard_map/reduce_scatter | solution.py:652
  118.1 57.2 %copy-start.3 = (f32[128,128,1]{1,0,2:T(8,128)S(1)}, f32[128,128,1]{1,0,2:T(8,128)}, u32[]{:S(2)}) copy-start(f32[128,128,1]{1,0,2:T(8,128)} %constant.63) | copy-start | bytes 196612
  118.1 57.9 %copy-start.4 = (f32[128,128,1]{1,0,2:T(8,128)S(1)}, f32[128,128,1]{1,0,2:T(8,128)}, u32[]{:S(2)}) copy-start(f32[128,128,1]{1,0,2:T(8,128)} %constant.62) | copy-start | bytes 196612
  179.0 5.3 %copy-start.5 = (f32[128]{0:T(128)S(1)}, f32[128]{0:T(128)}, u32[]{:S(2)}) copy-start(f32[128]{0:T(128)} %constant.54.clone) | copy-start | bytes 1540
  180.4 26.5 %all-to-all-start.1 = ((f32[2,128,8,128]{3,2,0,1:T(8,128)}), f32[2,128,8,128]{3,2,0,1:T(8,128)S(1)}, u32[]{:S(2)}, u32[]{:S(2)}) async-start(f32[2,128,8,128]{3,2,0,1:T(8,128)} %copy.61), calls=%async_computation.2 | async-start | bytes 2097152 | tf_op jit(solution)/shard_map/all_to_all | solution.py:606
  184.1 124.9 %all-gather.2.cloned.1.call-start = ((), (), s32[]{:S(2)}) async-start(), calls=%async_computation.6 | async-start | bytes 2621440 | tf_op jit(solution)/shard_map/all_gather | solution.py:656
  210.2 1.1 copy-start.1
  210.2 1.7 copy-start.2
  250.7 58.3 %copy-start = (f32[32,128,128]{2,1,0:T(8,128)S(1)}, f32[32,128,128]{2,1,0:T(8,128)}, u32[]{:S(2)}) copy-start(f32[32,128,128]{2,1,0:T(8,128)} %param.31) | copy-start | bytes 6291460
Sparse Core Ops, SparseCore 0:
  118.2 44.3 reduce-scatter.1
  263.9 45.0 all-gather.1

commit v2 on v1

--- a/solution.py
+++ b/solution.py
@@ -256,85 +256,180 @@
     return jnp.concatenate([high, low], 0)
 
 
+def split_three(values):
+    high = values.astype(jnp.bfloat16)
+    rest = values - high.astype(jnp.float32)
+    middle = rest.astype(jnp.bfloat16)
+    low = (rest - middle.astype(jnp.float32)).astype(jnp.bfloat16)
+    return [high, middle, low]
+
+
+def six_table(table):
+    parts, rest = [], np.asarray(table, np.float32)
+    for _ in range(3):
+        parts.append(rest.astype(ml_dtypes.bfloat16).astype(np.float32))
+        rest = rest - parts[-1]
+    high, middle, low = parts
+    return np.concatenate([high, high, high, middle, middle, low], 1).astype(ml_dtypes.bfloat16)
+
+
+def six_parts(values):
+    high, middle, low = split_three(values)
+    return [high, middle, low, high, middle, high]
+
+
+def exact_left(table_ref, values):
+    return dot(table_ref[...], jnp.concatenate(six_parts(values), 0))
+
+
+def exact_right(values, table_ref):
+    parts = six_parts(values)
+    width = values.shape[1]
+    total = None
+    for pair in range(3):
+        data = jnp.concatenate(parts[2 * pair : 2 * pair + 2], 1)
+        term = dot(data, table_ref[2 * pair * width : 2 * (pair + 1) * width, :])
+        total = term if total is None else total + term
+    return total
+
+
+def real_basis(length):
+    ids = np.arange(length)
+    angle = 2.0 * np.pi * ((ids[:, None] * ids[None, :]) % length) / length
+    table = np.where(ids[None, :] <= length // 2, np.cos(angle), np.sin(angle))
+    single = (ids == 0) | (2 * ids == length)
+    return table * np.where(single, 1.0, math.sqrt(2.0))[None, :] / math.sqrt(length)
+
+
+def rows_at(ref, row):
+    return ref[pl.ds(row, ref.shape[0] // LANE_ROWS, stride=LANE_ROWS), :]
+
+
+def put_rows(ref, row, values):
+    ref[pl.ds(row, ref.shape[0] // LANE_ROWS, stride=LANE_ROWS), :] = values
+
+
+def tile_of(index):
+    return pl.ds(pl.multiple_of(index * LANE_ROWS, LANE_ROWS), LANE_ROWS)
+
+
 def evolve_kernel(
     layers, far_rows, far, near_rows, lag,
-    weight_ref, psi_ref, wz_ref, wy_ref, gather_ref, spread_ref,
-    out_ref, density_ref,
+    weight_ref, wave_ref, psi_ref, local_ref, wz_ref, wy_ref, gather_ref, spread_ref,
+    qz_ref, qzt_ref, qy_ref, qyt_ref, qx_ref, qxt_ref, plane_wave_ref,
+    out_ref, angle_ref,
     stage, phi, give_far, give_near, got_far, got_near, far_field, result, density,
-    in_sem, out_sem, p_send, p_recv, q_send, q_recv, y_send, y_recv, f_send, f_recv, density_sem,
+    outer_sum, middle_sum, total, spectrum, lines, returned, local,
+    in_sem, out_sem, p_send, p_recv, q_send, q_recv, y_send, y_recv, f_send, f_recv,
+    a_send, a_recv, m_send, m_recv, t_send, t_recv, l_send, l_recv, b_send, b_recv, d_send, d_recv, v_sem,
 ):
     _, _, planes, ny, nz = psi_ref.shape
     groups = ny // LANE_ROWS
     tiles = groups // 2
     units = layers * tiles
-    bx = planes // tiles
+    bx = stage.shape[2]
+    per_layer = planes // bx
+    steps = layers * per_layer
+    paired = (layers - 3) * tiles
     place = lax.axis_index("grid")
     core = lax.rem(place, 2)
     sibling = place + 1 - 2 * core
     across = lax.rem(place + 2, 4)
+    depth = lax.axis_index("orb")
+    outer = (depth == 0) | (depth == 3)
+    inner = (depth == 1) | (depth == 2)
+    toward = 1 + depth // 3
+    outward = jnp.where(depth == 1, 0, 3)
+    middle = jnp.where(depth == 1, 2, 1)
+
+    def where_is(unit):
+        late = unit - paired
+        layer = jnp.where(late < 0, unit // tiles, layers - 3 + lax.rem(jnp.maximum(late, 0), 3))
+        tile = jnp.where(late < 0, lax.rem(unit, tiles), jnp.maximum(late, 0) // 3)
+        return layer, tile
+
+    def remote(source, target, send_sem, recv_sem, device):
+        return pltpu.make_async_remote_copy(
+            src_ref=source, dst_ref=target, send_sem=send_sem, recv_sem=recv_sem,
+            device_id=device, device_id_type=MESH,
+        )
 
     def far_copy(unit):
-        return pltpu.make_async_remote_copy(
-            src_ref=give_far.at[lax.rem(unit, 4), 1 - core], dst_ref=got_far.at[unit],
-            send_sem=p_send.at[unit], recv_sem=p_recv.at[unit],
-            device_id={"grid": sibling}, device_id_type=MESH,
+        return remote(
+            give_far.at[lax.rem(unit, 4), 1 - core], got_far.at[unit],
+            p_send.at[unit], p_recv.at[unit], {"grid": sibling},
         )
 
     def near_copy(unit):
-        return pltpu.make_async_remote_copy(
-            src_ref=give_near.at[lax.rem(unit, 4)], dst_ref=got_near.at[unit],
-            send_sem=q_send.at[unit], recv_sem=q_recv.at[unit],
-            device_id={"grid": sibling}, device_id_type=MESH,
+        return remote(
+            give_near.at[lax.rem(unit, 4)], got_near.at[unit],
+            q_send.at[unit], q_recv.at[unit], {"grid": sibling},
         )
 
     def across_copy(unit):
-        return pltpu.make_async_remote_copy(
-            src_ref=got_far.at[unit], dst_ref=far_field.at[unit, core, pl.ds(0, far_rows)],
-            send_sem=y_send.at[unit], recv_sem=y_recv.at[unit],
-            device_id={"grid": across}, device_id_type=MESH,
+        return remote(
+            got_far.at[unit], far_field.at[unit, core, pl.ds(0, far_rows * LANE_ROWS)],
+            y_send.at[unit], y_recv.at[unit], {"grid": across},
         )
 
     def share_copy(unit):
-        held = far_field.at[unit, core, pl.ds(0, far_rows)]
-        return pltpu.make_async_remote_copy(
-            src_ref=held, dst_ref=held,
-            send_sem=f_send.at[unit], recv_sem=f_recv.at[unit],
-            device_id={"grid": sibling}, device_id_type=MESH,
-        )
+        held = far_field.at[unit, core, pl.ds(0, far_rows * LANE_ROWS)]
+        return remote(held, held, f_send.at[unit], f_recv.at[unit], {"grid": sibling})
+
+    def outer_copy(g):
+        return remote(density.at[g], outer_sum.at[g], a_send.at[g], a_recv.at[g], {"orb": toward})
+
+    def middle_copy(g):
+        return remote(density.at[g], middle_sum.at[g], m_send.at[g], m_recv.at[g], {"orb": middle})
+
+    def total_copy(g):
+        return remote(total.at[g], total.at[g], t_send.at[g], t_recv.at[g], {"orb": outward})
 
     def load_copy(step):
-        layer, part = step // tiles, lax.rem(step, tiles)
+        layer, part = step // per_layer, lax.rem(step, per_layer)
         slot = lax.rem(step, 3)
         return pltpu.make_async_copy(
             psi_ref.at[layer, :, pl.ds(part * bx, bx)], stage.at[slot], in_sem.at[slot]
         )
 
     def result_copy(unit, half):
-        layer, tile = unit // tiles, lax.rem(unit, tiles)
+        layer, tile = where_is(unit)
         slot = lax.rem(unit, 3)
-        row = pl.multiple_of((2 * tile + half) * LANE_ROWS, LANE_ROWS)
         return pltpu.make_async_copy(
             result.at[slot, half],
-            out_ref.at[layer, :, pl.ds(row, LANE_ROWS), :],
+            out_ref.at[layer, 2 * tile + half],
             out_sem.at[slot, half],
         )
 
     load_copy(0).start()
     load_copy(1).start()
+    local_copy = pltpu.make_async_copy(local_ref, local, v_sem)
+    local_copy.start()
     if far > far_rows:
-        far_field[:, :, far_rows:] = jnp.zeros((units, 2, far - far_rows, LANE_ROWS, nz), jnp.float32)
+        far_field[:, :, far_rows * LANE_ROWS :] = jnp.zeros((units, 2, (far - far_rows) * LANE_ROWS, nz), jnp.float32)
+    density[...] = jnp.zeros_like(density)
     barrier = pltpu.get_barrier_semaphore()
-    for peer in (sibling, across):
-        pl.semaphore_signal(barrier, inc=1, device_id={"grid": peer}, device_id_type=MESH)
-    pl.semaphore_wait(barrier, 2)
-
-    def plane_step(step):
-        @pl.when(step + 2 < units)
+    for k in range(1, 4):
+        pl.semaphore_signal(barrier, inc=1, device_id={"grid": lax.rem(place + k, 4)}, device_id_type=MESH)
+
+    @pl.when(outer)
+    def _():
+        pl.semaphore_signal(barrier, inc=1, device_id={"orb": toward}, device_id_type=MESH)
+        pl.semaphore_wait(barrier, 4)
+
+    @pl.when(inner)
+    def _():
+        pl.semaphore_signal(barrier, inc=1, device_id={"orb": outward}, device_id_type=MESH)
+        pl.semaphore_signal(barrier, inc=1, device_id={"orb": middle}, device_id_type=MESH)
+        pl.semaphore_wait(barrier, 5)
+
+    def plane_step(step, carry):
+        @pl.when(step + 2 < steps)
         def _():
             load_copy(step + 2).start()
 
         load_copy(step).wait()
-        layer, part = step // tiles, lax.rem(step, tiles)
+        layer, part = step // per_layer, lax.rem(step, per_layer)
         slot = lax.rem(step, 3)
         real_part = stage[slot, 0].reshape(bx * ny, nz)
         imag_part = stage[slot, 1].reshape(bx * ny, nz)
@@ -347,10 +442,11 @@
         for c in range(2):
             for p in range(bx):
                 block = rows[c * ny : (c + 1) * ny, p * nz : (p + 1) * nz]
-                phi[layer, :, c * planes + part * bx + p] = block.reshape(groups, LANE_ROWS, nz)
+                phi[layer, :, tile_of(c * planes + part * bx + p), :] = block.reshape(groups, LANE_ROWS, nz)
+        return carry
 
     def gather_step(unit):
-        layer, tile = unit // tiles, lax.rem(unit, tiles)
+        layer, tile = where_is(unit)
         slot = lax.rem(unit, 4)
 
         @pl.when(unit >= 4)
@@ -361,20 +457,21 @@
         for half in range(2):
             for part in range(2):
                 ids = range(4 * part, 4 * part + 4)
-                data = jnp.concatenate([phi[layer, 2 * tile + half, :, i, :] for i in ids], 1)
+                source = phi.at[layer, 2 * tile + half]
+                data = jnp.concatenate([rows_at(source, i) for i in ids], 1)
                 both = dot(gather_ref[core], stack_split(data))
-                total = both[: far + near_rows] + both[far + near_rows :]
+                joined = both[: far + near_rows] + both[far + near_rows :]
                 for k, i in enumerate(ids):
-                    block = total[:, k * nz : (k + 1) * nz]
-                    give_far[slot, half, :, i, :] = block[:far_rows]
-                    give_near[slot, half, :, i, :] = block[far:]
+                    block = joined[:, k * nz : (k + 1) * nz]
+                    put_rows(give_far.at[slot, half], i, block[:far_rows])
+                    put_rows(give_near.at[slot, half], i, block[far:])
 
     def sum_step(unit):
         far_copy(unit).wait_recv()
         got_far[unit] = got_far[unit] + give_far[lax.rem(unit, 4), core]
 
     def spread_step(unit):
-        layer, tile = unit // tiles, lax.rem(unit, tiles)
+        layer, tile = where_is(unit)
         slot = lax.rem(unit, 3)
         near_copy(unit).wait_recv()
         share_copy(unit).wait_recv()
@@ -392,9 +489,9 @@
                     [
                         jnp.concatenate(
                             [
-                                phi[layer, 2 * tile + half, :, i, :],
-                                got_near[unit, half, :, i, :],
-                                far_field[unit, half, :, i, :],
+                                rows_at(phi.at[layer, 2 * tile + half], i),
+                                rows_at(got_near.at[unit, half], i),
+                                rows_at(far_field.at[unit, half], i),
                             ],
                             0,
                         )
@@ -407,14 +504,45 @@
                 squares = moved * moved
                 term = weight * (squares[:planes] + squares[planes:])
                 for k, i in enumerate(ids):
-                    result[slot, half, :, i, :] = moved[:, k * nz : (k + 1) * nz]
-                    earlier = density[2 * tile + half, :, i, :]
-                    value = term[:, k * nz : (k + 1) * nz]
-                    density[2 * tile + half, :, i, :] = value + jnp.where(layer == 0, 0.0, earlier)
-
-    first_gather = tiles
-    first_forward = tiles + 3 + lag
+                    put_rows(result.at[slot, half], i, moved[:, k * nz : (k + 1) * nz])
+                    summed = density.at[2 * tile + half]
+                    put_rows(summed, i, rows_at(summed, i) + term[:, k * nz : (k + 1) * nz])
+
+    def send(unit):
+        far_copy(unit).start()
+        near_copy(unit).start()
+
+    def forward(unit):
+        across_copy(unit).wait_recv()
+        share_copy(unit).start()
+
+    def write(unit):
+        result_copy(unit, 0).start()
+        result_copy(unit, 1).start()
+
+    def add_outer(g):
+        outer_copy(g).wait_recv()
+        density[g] = density[g] + outer_sum[g]
+
+    def add_middle(g):
+        middle_copy(g).wait_recv()
+        total[g] = density[g] + middle_sum[g]
+
+    def flatten(g):
+        outer_sum[g] = exact_right(total[g], qz_ref)
+
+    def receive(g):
+        total_copy(g).wait_recv()
+        flatten(g)
+
+    def prepared(t):
+        late = jnp.maximum(t - 2, 0)
+        return jnp.minimum(per_layer + (late * (layers - 1) * per_layer) // (paired - 2), steps)
+
+    first_forward = 3 + lag
     first_spread = first_forward + 2
+    ready = first_spread + 1
+    last = ready + 15
 
     def tick(t, carry):
         def stage_at(start, action):
@@ -424,35 +552,122 @@
             def _():
                 action(unit)
 
-        def send(unit):
-            far_copy(unit).start()
-            near_copy(unit).start()
-
-        def forward(unit):
-            across_copy(unit).wait_recv()
-            share_copy(unit).start()
-
-        def write(unit):
-            result_copy(unit, 0).start()
-            result_copy(unit, 1).start()
-
-        stage_at(first_gather + 1, send)
-        stage_at(first_gather + 3, lambda unit: across_copy(unit).start())
-        stage_at(first_spread + 1, write)
-        stage_at(0, plane_step)
-        stage_at(first_gather + 2, sum_step)
-        stage_at(first_gather, gather_step)
+        def reduce_at(start, who, action):
+            late = t - start - paired
+
+            @pl.when((late >= 0) & (late < 3 * tiles) & (lax.rem(late + 3 * units, 3) == 2) & who)
+            def _():
+                action(2 * (late // 3))
+                action(2 * (late // 3) + 1)
+
+        stage_at(1, send)
+        stage_at(3, lambda unit: across_copy(unit).start())
+        stage_at(ready, write)
+        reduce_at(ready, outer, lambda g: outer_copy(g).start())
+        reduce_at(ready + 4, inner, add_outer)
+        reduce_at(ready + 5, inner, lambda g: middle_copy(g).start())
+        reduce_at(ready + 9, inner, add_middle)
+        reduce_at(ready + 10, inner, lambda g: total_copy(g).start())
+        reduce_at(ready + 10, inner, flatten)
+        reduce_at(ready + 15, outer, receive)
+        lax.fori_loop(prepared(t), prepared(t + 1), plane_step, 0)
+        stage_at(2, sum_step)
+        stage_at(0, gather_step)
         stage_at(first_forward, forward)
         stage_at(first_spread, spread_step)
         return carry
 
-    density[...] = jnp.zeros_like(density)
-    lax.fori_loop(0, first_spread + 1 + units, tick, 0)
-
-    for g in range(groups):
-        pltpu.make_async_copy(
-            density.at[g], density_ref.at[:, pl.ds(g * LANE_ROWS, LANE_ROWS), :], density_sem.at[g]
-        ).start()
+    lax.fori_loop(0, per_layer, plane_step, 0)
+    lax.fori_loop(0, last + units, tick, 0)
+
+    local_copy.wait()
+
+    four = 4
+
+    def spectrum_step(part, carry):
+        ids = [part * four + p for p in range(four)]
+        moved = exact_left(
+            qyt_ref, jnp.concatenate([outer_sum[:, tile_of(x), :].reshape(ny, nz) for x in ids], 1)
+        )
+        for p, x in enumerate(ids):
+            spectrum[:, tile_of(x), :] = moved[:, p * nz : (p + 1) * nz].reshape(groups, LANE_ROWS, nz)
+        return carry
+
+    lax.fori_loop(0, planes // four, spectrum_step, 0)
+    share = groups // 8
+    span = planes * LANE_ROWS
+    mine = lax.rem(depth, 2) * (groups // 2)
+    other = groups // 2 - mine
+    partner = depth + 1 - 2 * lax.rem(depth, 2)
+
+    def lines_of(device):
+        return pl.ds(pl.multiple_of(device * span, span), span)
+
+    def line_copy(g, k):
+        peer = lax.rem(place + k, 4)
+        return remote(
+            spectrum.at[mine + peer * share + g], lines.at[g, lines_of(place)],
+            l_send.at[g, k - 1], l_recv.at[g, k - 1], {"grid": peer},
+        )
+
+    def back_copy(g, k):
+        peer = lax.rem(place + k, 4)
+        return remote(
+            lines.at[g, lines_of(peer)], returned.at[mine + place * share + g],
+            b_send.at[g, k - 1], b_recv.at[g, k - 1], {"grid": peer},
+        )
+
+    def pair_copy(row):
+        return remote(
+            returned.at[row], returned.at[row],
+            d_send.at[row], d_recv.at[row], {"orb": partner},
+        )
+
+    for g in range(share):
+        for k in (2, 3, 1):
+            line_copy(g, k).start()
+        lines[g, lines_of(place)] = spectrum[mine + place * share + g]
+
+    for g in range(share):
+        for k in (1, 2, 3):
+            line_copy(g, k).wait_recv()
+        for part in range(2):
+            ids = range(4 * part, 4 * part + 4)
+            data = jnp.concatenate([rows_at(lines.at[g], i) for i in ids], 1)
+            modes = exact_left(qxt_ref, data)
+            scaled = []
+            for k, i in enumerate(ids):
+                waves = plane_wave_ref[...] + wave_ref[(mine + place * share + g) * LANE_ROWS + i]
+                anchor = waves <= 0.0
+                kernel = jnp.where(anchor, 0.0, HARTREE_SCALE / jnp.where(anchor, 1.0, waves))
+                scaled.append(modes[:, k * nz : (k + 1) * nz] * kernel)
+            moved = exact_left(qx_ref, jnp.concatenate(scaled, 1))
+            for k, i in enumerate(ids):
+                put_rows(lines.at[g], i, moved[:, k * nz : (k + 1) * nz])
+        if g > 0:
+            for k in (2, 3, 1):
+                back_copy(g - 1, k).start()
+    for k in (2, 3, 1):
+        back_copy(share - 1, k).start()
+    for g in range(share):
+        returned[mine + place * share + g] = lines[g, lines_of(place)]
+    for g in range(share):
+        for k in (1, 2, 3):
+            line_copy(g, k).wait_send()
+
+    def straighten(row):
+        spectrum[row] = exact_right(returned[row], qzt_ref)
+
+    for g in range(share):
+        pair_copy(mine + place * share + g).start()
+    for g in range(share):
+        straighten(mine + place * share + g)
+    for g in range(share):
+        for k in (3, 1, 2):
+            row = mine + lax.rem(place + 4 - k, 4) * share + g
+            back_copy(g, k).wait_recv()
+            pair_copy(row).start()
+            straighten(row)
 
     def finish(unit, carry):
         across_copy(unit).wait_send()
@@ -471,75 +686,148 @@
         return carry
 
     lax.fori_loop(0, units, finish, 0)
-    for g in range(groups):
-        pltpu.make_async_copy(
-            density.at[g], density_ref.at[:, pl.ds(g * LANE_ROWS, LANE_ROWS), :], density_sem.at[g]
-        ).wait()
-
-
-def evolve(orbitals, weights, wz, wy):
+
+    @pl.when(outer)
+    def _():
+        for g in range(groups):
+            outer_copy(g).wait_send()
+
+    @pl.when(inner)
+    def _():
+        for g in range(groups):
+            middle_copy(g).wait_send()
+            total_copy(g).wait_send()
+
+    for k in (0, 3, 1, 2):
+        for g in range(share):
+            row = other + lax.rem(place + 4 - k, 4) * share + g
+            pair_copy(row).wait_recv()
+            straighten(row)
+
+    def potential_step(part, carry):
+        ids = [part * four + p for p in range(four)]
+        moved = exact_left(
+            qy_ref, jnp.concatenate([spectrum[:, tile_of(x), :].reshape(ny, nz) for x in ids], 1)
+        )
+        for p, x in enumerate(ids):
+            angle_ref[x] = TIME_STEP * (local[x] + moved[:, p * nz : (p + 1) * nz])
+        return carry
+
+    lax.fori_loop(0, planes // four, potential_step, 0)
+    for g in range(share):
+        for k in (1, 2, 3):
+            back_copy(g, k).wait_send()
+
+    def settle(row, carry):
+        pair_copy(mine + row).wait_send()
+        return carry
+
+    lax.fori_loop(0, groups // 2, settle, 0)
+
+
+def evolve(orbitals, v_local, weights, wz, wy):
     layers, _, planes, ny, nz = orbitals.shape
-    gather, spread, far_rows, far, near_rows = evolve_tables(4 * planes, planes)
+    width_x = 4 * planes
+    gather, spread, far_rows, far, near_rows = evolve_tables(width_x, planes)
     groups = ny // LANE_ROWS
-    units = layers * groups // 2
+    tiles = groups // 2
+    units = layers * tiles
     f32 = jnp.float32
+    squares = [wave_squared(n).astype(np.float32) for n in (width_x, ny, nz)]
+    plane_wave = squares[0][:, None] + squares[2][None, :]
+    basis = [real_basis(n) for n in (width_x, ny, nz)]
+    tables = [
+        six_table(basis[2].T).T, six_table(basis[2]).T, six_table(basis[1]), six_table(basis[1].T),
+        six_table(basis[0]), six_table(basis[0].T), plane_wave,
+    ]
     vmem = pl.BlockSpec(memory_space=pltpu.VMEM)
+    smem = pl.BlockSpec(memory_space=pltpu.SMEM)
     anywhere = pl.BlockSpec(memory_space=pl.ANY)
     dma = pltpu.SemaphoreType.DMA
-    evolved, density = pl.pallas_call(
+    field = pltpu.VMEM((groups, planes * LANE_ROWS, nz), f32)
+    evolved, angle = pl.pallas_call(
         partial(evolve_kernel, layers, far_rows, far, near_rows, 3),
-        in_specs=[pl.BlockSpec(memory_space=pltpu.SMEM), anywhere, vmem, vmem, vmem, vmem],
-        out_specs=[anywhere, anywhere],
+        in_specs=[smem, smem, anywhere, anywhere] + [vmem] * 11,
+        out_specs=[anywhere, vmem],
         out_shape=[
-            jax.ShapeDtypeStruct((layers, 2 * planes, ny, nz), f32),
+            jax.ShapeDtypeStruct((layers, groups, 2 * planes * LANE_ROWS, nz), f32),
             jax.ShapeDtypeStruct((planes, ny, nz), f32),
         ],
         scratch_shapes=[
-            pltpu.VMEM((3, 2, planes * 2 // groups, ny, nz), f32),
-            pltpu.VMEM((layers, groups, 2 * planes, LANE_ROWS, nz), f32),
-            pltpu.VMEM((4, 2, far_rows, LANE_ROWS, nz), f32),
-            pltpu.VMEM((4, 2, near_rows, LANE_ROWS, nz), f32),
-            pltpu.VMEM((units, far_rows, LANE_ROWS, nz), f32),
-            pltpu.VMEM((units, 2, near_rows, LANE_ROWS, nz), f32),
-            pltpu.VMEM((units, 2, far, LANE_ROWS, nz), f32),
-            pltpu.VMEM((3, 2, 2 * planes, LANE_ROWS, nz), f32),
-            pltpu.VMEM((groups, planes, LANE_ROWS, nz), f32),
+            pltpu.VMEM((3, 2, 8, ny, nz), f32),
+            pltpu.VMEM((layers, groups, 2 * planes * LANE_ROWS, nz), f32),
+            pltpu.VMEM((4, 2, far_rows * LANE_ROWS, nz), f32),
+            pltpu.VMEM((4, 2, near_rows * LANE_ROWS, nz), f32),
+            pltpu.VMEM((units, far_rows * LANE_ROWS, nz), f32),
+            pltpu.VMEM((units, 2, near_rows * LANE_ROWS, nz), f32),
+            pltpu.VMEM((units, 2, far * LANE_ROWS, nz), f32),
+            pltpu.VMEM((3, 2, 2 * planes * LANE_ROWS, nz), f32),
+            field, field, field, field, field,
+            pltpu.VMEM((groups // 8, width_x * LANE_ROWS, nz), f32),
+            field,
+            pltpu.VMEM((planes, ny, nz), f32),
             dma((3,)),
             dma((3, 2)),
         ]
         + [dma((units,))] * 8
-        + [dma((groups,))],
+        + [dma((groups,))] * 6
+        + [dma((groups // 8, 3))] * 4
+        + [dma((groups,))] * 2
+        + [pltpu.SemaphoreType.DMA],
         compiler_params=pltpu.CompilerParams(
-            vmem_limit_bytes=60 * 1024 * 1024, collective_id=0, has_side_effects=True
+            vmem_limit_bytes=63 * 1024 * 1024, collective_id=0, has_side_effects=True
         ),
         cost_estimate=pl.CostEstimate(
             flops=40 * layers * planes * ny * nz * (ny + nz), bytes_accessed=16 * layers * planes * ny * nz, transcendentals=0
         ),
-    )(weights, orbitals, wz, wy, jnp.asarray(gather), jnp.asarray(spread))
-    return evolved.reshape(layers, 2, planes, ny, nz), density
-
-
-def turn_kernel(psi_ref, cos_ref, sin_ref, out_ref):
-    cosine, sine = cos_ref[...], sin_ref[...]
-    for l in range(psi_ref.shape[0]):
-        real_part, imag_part = psi_ref[l, 0], psi_ref[l, 1]
-        out_ref[l, 0] = real_part * cosine + imag_part * sine
-        out_ref[l, 1] = imag_part * cosine - real_part * sine
-
-
-def turn(evolved, cosine, sine):
-    layers, _, planes, ny, nz = evolved.shape
+    )(weights, jnp.asarray(squares[1]), orbitals, v_local, wz, wy, *map(jnp.asarray, [gather, spread] + tables))
+    return evolved.reshape(layers, groups, 2, planes, LANE_ROWS, nz), angle
+
+
+def cos_sin(angle):
+    turns = jnp.floor(angle * (2.0 / math.pi) + 0.5)
+    rest = ((angle - turns * 1.5703125) - turns * 4.837512969970703125e-4) - turns * 7.549789954891882e-8
+    square = rest * rest
+    sine = ((-1.9515295891e-4 * square + 8.3321608736e-3) * square - 1.6666654611e-1) * square * rest + rest
+    cosine = (
+        (2.443315711809948e-5 * square - 1.388731625493765e-3) * square + 4.166664568298827e-2
+    ) * square * square - 0.5 * square + 1.0
+    quarter = turns.astype(jnp.int32) & 3
+    odd = (quarter & 1) == 1
+    first = jnp.where(odd, sine, cosine)
+    second = jnp.where(odd, cosine, sine)
+    first = jnp.where((quarter == 1) | (quarter == 2), -first, first)
+    second = jnp.where(quarter >= 2, -second, second)
+    return first, second
+
+
+def turn_kernel(psi_ref, angle_ref, out_ref):
+    cosine, sine = cos_sin(angle_ref[...])
+    for g in range(psi_ref.shape[1]):
+        band = slice(g * LANE_ROWS, (g + 1) * LANE_ROWS)
+        turn_re, turn_im = cosine[:, band], sine[:, band]
+        for l in range(psi_ref.shape[0]):
+            real_part, imag_part = psi_ref[l, g, 0], psi_ref[l, g, 1]
+            out_ref[l, 0, :, band, :] = real_part * turn_re + imag_part * turn_im
+            out_ref[l, 1, :, band, :] = imag_part * turn_re - real_part * turn_im
+
+
+def turn(evolved, angle):
+    layers, groups, _, planes, _, nz = evolved.shape
+    ny = groups * LANE_ROWS
     bx = min(4, planes)
     field_block = pl.BlockSpec((bx, ny, nz), lambda i: (i, 0, 0))
-    block = pl.BlockSpec((layers, 2, bx, ny, nz), lambda i: (0, 0, i, 0, 0))
     return pl.pallas_call(
         turn_kernel,
         grid=(planes // bx,),
-        in_specs=[block, field_block, field_block],
-        out_specs=block,
-        out_shape=jax.ShapeDtypeStruct(evolved.shape, jnp.float32),
+        in_specs=[
+            pl.BlockSpec((layers, groups, 2, bx, LANE_ROWS, nz), lambda i: (0, 0, 0, i, 0, 0)),
+            field_block,
+        ],
+        out_specs=pl.BlockSpec((layers, 2, bx, ny, nz), lambda i: (0, 0, i, 0, 0)),
+        out_shape=jax.ShapeDtypeStruct((layers, 2, planes, ny, nz), jnp.float32),
         compiler_params=pltpu.CompilerParams(vmem_limit_bytes=VMEM_LIMIT),
-    )(evolved, cosine, sine)
+    )(evolved, angle)
 
 
 def rotate_kernel(layers, *refs):
@@ -596,7 +884,7 @@
     return jnp.where(anchor, 0.0, HARTREE_SCALE / jnp.where(anchor, 1.0, total))
 
 
-def poisson_shared(density, names):
+def poisson_shared(density):
     width_x, _, count_z = density.shape
     span_count = lax.axis_size("grid") * lax.axis_size("orb")
     block_x = width_x // span_count
@@ -605,14 +893,14 @@
     real_part, imag_part = complex_along(real_part, imag_part, fourier(width_x, -1), 0)
     spread = lax.all_to_all(
         jnp.stack([real_part, imag_part], 0),
-        names,
+        ("grid", "orb"),
         split_axis=1,
         concat_axis=2,
         tiled=True,
     )
     count_y = spread.shape[2]
     real_part, imag_part = complex_along(spread[0], spread[1], fourier(count_y, -1), 1)
-    start_x = lax.axis_index(names) * block_x
+    start_x = lax.axis_index(("grid", "orb")) * block_x
     squares_x = lax.dynamic_slice_in_dim(
         jnp.asarray(wave_squared(width_x), jnp.float32), start_x, block_x, 0
     )
@@ -626,7 +914,7 @@
     )
     back = lax.all_to_all(
         jnp.stack([real_part, imag_part], 0),
-        names,
+        ("grid", "orb"),
         split_axis=2,
         concat_axis=1,
         tiled=True,
@@ -647,15 +935,17 @@
     order = np.arange(2 * width_x).reshape(2, grid_count, planes).transpose(1, 0, 2).reshape(-1)
     wx = jnp.asarray(split_const(left_block(kinetic_matrix(width_x))[order][:, order]))
     weights = lax.dynamic_slice_in_dim(occupations, lax.axis_index("orb") * layers, layers, 0)
-    if grid_count == 4 and 2 * planes % (count_y // LANE_ROWS) == 0 and count_y % (2 * LANE_ROWS) == 0:
-        evolved, density = evolve(orbitals, weights, wz, wy)
-        share = lax.psum_scatter(density, "orb", scatter_dimension=1, tiled=True)
-        lines = lax.all_to_all(share, "grid", split_axis=1, concat_axis=0, tiled=True)
-        hartree_lines = poisson_shared(lines, ("orb", "grid"))
-        rows_back = lax.all_to_all(hartree_lines, "grid", split_axis=0, concat_axis=1, tiled=True)
-        hartree = lax.all_gather(rows_back, "orb", axis=1, tiled=True)
-        angle = TIME_STEP * (v_local + hartree)
-        return turn(evolved, jnp.cos(angle), jnp.sin(angle))
+    if (
+        grid_count == 4
+        and orb_count == 4
+        and layers >= 4
+        and planes % 8 == 0
+        and count_y % (8 * LANE_ROWS) == 0
+        and count_z % 128 == 0
+    ):
+        evolved, angle = evolve(orbitals, v_local, weights, wz, wy)
+        return turn(evolved, angle)
+
     exchange = partial(lax.all_to_all, axis_name="grid", split_axis=0, concat_axis=0, tiled=True)
 
     received = [
@@ -670,7 +960,7 @@
         returned.append(exchange(moved))
     share = lax.psum_scatter(density, "orb", scatter_dimension=1, tiled=True)
     share, returned[0] = lax.optimization_barrier((share, returned[0]))
-    hartree_lines = poisson_shared(share, ("grid", "orb"))
+    hartree_lines = poisson_shared(share)
     rows_back = lax.all_to_all(hartree_lines, "grid", split_axis=0, concat_axis=1, tiled=True)
     gathered = lax.all_gather(rows_back, "orb", axis=0, tiled=False)
     hartree = gathered.reshape(orb_count, planes, grid_count, share_y, count_z)

time: 341 us -> 198 us (0.58)
  waiting for transfers between devices: 112 us -> 0 us
  Pallas kernels: 125 us -> 193 us
  blocking collectives: 54.4 us -> 0 us
  matrix products: 14.1 us -> 0 us
  between operations: 13.8 us -> 0.02 us
  other arithmetic: 9.74 us -> 0 us
  local copies, waits for them, and re-layouts: 6.92 us -> 2.82 us
  starting transfers between devices: 3.88 us -> 0 us
    pallas_call x1, Pallas kernels: 110 us -> 177 us  [evolve(): pl.pallas_call(partial(evolve_kernel, layers, far_rows, far, near_rows, 3...]
    all_to_all x3 -> x0, blocking collectives: 54.4 us -> none  [the longest x1 31.2 us: poisson_shared(): lax.all_to_all(jnp.stack([real_part, imag_part], 0), names, split_axis=2,...]
    all_gather x1 -> x0, waiting for transfers between devices: 45.2 us -> none  [body(): hartree = lax.all_gather(rows_back, 'orb', axis=1, tiled=True)]
    reduce_scatter x1 -> x0, waiting for transfers between devices: 44.5 us -> none  [body(): share = lax.psum_scatter(density, 'orb', scatter_dimension=1, tiled=True)]
    all_to_all x1 -> x0, waiting for transfers between devices: 22.5 us -> none  [poisson_shared(): lax.all_to_all(jnp.stack([real_part, imag_part], 0), names, split_axis=1,...]
    dot_general x20 -> x0, matrix products: 14.1 us -> none  [apply_along(): jnp.tensordot(values, table, axes=([axis], [0]), precision=HIGHEST)]
    sin x1 -> x0, other arithmetic: 9.52 us -> none  [body(): return turn(evolved, jnp.cos(angle), jnp.sin(angle))]
    all_to_all x1 -> x0, starting transfers between devices: 3.66 us -> none  [poisson_shared(): lax.all_to_all(jnp.stack([real_part, imag_part], 0), names, split_axis=1,...]
  transfers between devices with their start and end apart: 3 -> 0, of which waited for: 3 -> 0; matrix products, arithmetic and copies ran while one was open for 0% -> 0% of each run, Pallas kernels for 0% -> 0%
where the time goes in v2:
time: 198 us; the launch traced here: 196 us
  Pallas kernels  193 us (97%)
  local copies, waits for them, and re-layouts  2.82 us (1%)
    pallas_call x1, Pallas kernels, evolve(): pl.pallas_call(partial(evolve_kernel, layers, far_rows, far, near_rows, 3...  177 us
    pallas_call x1, Pallas kernels, turn(): pl.pallas_call(turn_kernel, grid=(planes // bx,), in_specs=[pl.BlockSpec(...  15.4 us

profile of v2, /device:TPU:0, one launch (start us, length us, event | category | flops | bytes accessed | tf_op | source)
XLA Modules:
  0.0 195.5 jit_solution(16947820111373277173)
XLA Ops:
  0.0 1.2 dynamic_slice.3.weight_ref
  1.2 177.2 %shard_map.145 = (f32[4,16,512,128]{3,2,1,0:T(8,128)}, f32[32,128,128]{2,1,0:T(8,128)}) custom-call(f32[4]{0:T(128)} %dynamic_slice.3.weight_ref, f32[128]{0:T(128)} %constant.32.clone.wave_ref, f32[4,2,32,128,128]{4,3,2,1,0:T(8,128)} %psi_ref.1, f32[32,128,128]{2,1,0:T(8,128)} %local_ref.1, bf16[2,256,256]{2,1,0:T(8,128)(2,1)} %constant.30.clone.wz_ref, ...), custom_call_target="tpu_custom_call" | custom-call | flops 21474836480 | bytes 33554432 | tf_op jit(solution)/shard_map/pallas_call | solution.py:748
  178.5 0.0 copy-start
  178.5 1.6 copy-done
  180.1 15.4 %shard_map.146 = f32[4,2,32,128,128]{4,3,2,1,0:T(8,128)} custom-call(f32[4,16,2,32,8,128]{5,4,3,2,1,0:T(8,128)} %bitcast.1, f32[32,128,128]{2,1,0:T(8,128)S(1)} %copy-done), custom_call_target="tpu_custom_call" | custom-call | tf_op jit(solution)/shard_map/pallas_call | solution.py:820
Async XLA Ops:
  178.5 1.6 copy-start

commit v3 on v2

--- a/solution.py
+++ b/solution.py
@@ -376,14 +376,27 @@
         held = far_field.at[unit, core, pl.ds(0, far_rows * LANE_ROWS)]
         return remote(held, held, f_send.at[unit], f_recv.at[unit], {"grid": sibling})
 
-    def outer_copy(g):
-        return remote(density.at[g], outer_sum.at[g], a_send.at[g], a_recv.at[g], {"orb": toward})
-
-    def middle_copy(g):
-        return remote(density.at[g], middle_sum.at[g], m_send.at[g], m_recv.at[g], {"orb": middle})
-
-    def total_copy(g):
-        return remote(total.at[g], total.at[g], t_send.at[g], t_recv.at[g], {"orb": outward})
+    piece = planes * LANE_ROWS // 2
+
+    def piece_of(ref, g, p):
+        return ref.at[g, pl.ds(p * piece, piece)]
+
+    def outer_copy(g, p):
+        return remote(
+            piece_of(density, g, p), piece_of(outer_sum, g, p), a_send.at[g, p], a_recv.at[g, p], {"orb": toward}
+        )
+
+    def middle_copy(g, p):
+        return remote(
+            piece_of(density, g, p), piece_of(middle_sum, g, p), m_send.at[g, p], m_recv.at[g, p], {"orb": middle}
+        )
+
+    def total_copy(g, p):
+        held = piece_of(total, g, p)
+        return remote(held, held, t_send.at[g, p], t_recv.at[g, p], {"orb": outward})
+
+    def pieces(tile):
+        return [(2 * tile + g, p) for g in range(2) for p in range(2)]
 
     def load_copy(step):
         layer, part = step // per_layer, lax.rem(step, per_layer)
@@ -415,13 +428,11 @@
     @pl.when(outer)
     def _():
         pl.semaphore_signal(barrier, inc=1, device_id={"orb": toward}, device_id_type=MESH)
-        pl.semaphore_wait(barrier, 4)
 
     @pl.when(inner)
     def _():
         pl.semaphore_signal(barrier, inc=1, device_id={"orb": outward}, device_id_type=MESH)
         pl.semaphore_signal(barrier, inc=1, device_id={"orb": middle}, device_id_type=MESH)
-        pl.semaphore_wait(barrier, 5)
 
     def plane_step(step, carry):
         @pl.when(step + 2 < steps)
@@ -481,7 +492,7 @@
             result_copy(unit - 3, 0).wait()
             result_copy(unit - 3, 1).wait()
 
-        weight = weight_ref[layer]
+        weight = weight_ref[depth * layers + layer]
         for half in range(2):
             for part in range(2):
                 ids = range(4 * part, 4 * part + 4)
@@ -520,20 +531,46 @@
         result_copy(unit, 0).start()
         result_copy(unit, 1).start()
 
-    def add_outer(g):
-        outer_copy(g).wait_recv()
-        density[g] = density[g] + outer_sum[g]
-
-    def add_middle(g):
-        middle_copy(g).wait_recv()
-        total[g] = density[g] + middle_sum[g]
+    def start_outer(tile):
+        for g, p in pieces(tile):
+            outer_copy(g, p).start()
+
+    def add_outer(tile):
+        held = None
+        for g, p in pieces(tile):
+            outer_copy(g, p).wait_recv()
+            rows = pl.ds(p * piece, piece)
+            density[g, rows] = density[g, rows] + outer_sum[g, rows]
+            if held is not None:
+                middle_copy(*held).start()
+            held = (g, p)
+
+    def start_middle(tile):
+        middle_copy(2 * tile + 1, 1).start()
+
+    def add_middle(tile):
+        held = None
+        for g, p in pieces(tile):
+            middle_copy(g, p).wait_recv()
+            rows = pl.ds(p * piece, piece)
+            total[g, rows] = density[g, rows] + middle_sum[g, rows]
+            if held is not None:
+                total_copy(*held).start()
+            held = (g, p)
+
+    def start_total(tile):
+        total_copy(2 * tile + 1, 1).start()
+        for g in range(2):
+            flatten(2 * tile + g)
 
     def flatten(g):
         outer_sum[g] = exact_right(total[g], qz_ref)
 
-    def receive(g):
-        total_copy(g).wait_recv()
-        flatten(g)
+    def receive(tile):
+        for g in range(2):
+            for p in range(2):
+                total_copy(2 * tile + g, p).wait_recv()
+            flatten(2 * tile + g)
 
     def prepared(t):
         late = jnp.maximum(t - 2, 0)
@@ -557,18 +594,16 @@
 
             @pl.when((late >= 0) & (late < 3 * tiles) & (lax.rem(late + 3 * units, 3) == 2) & who)
             def _():
-                action(2 * (late // 3))
-                action(2 * (late // 3) + 1)
+                action(late // 3)
 
         stage_at(1, send)
         stage_at(3, lambda unit: across_copy(unit).start())
         stage_at(ready, write)
-        reduce_at(ready, outer, lambda g: outer_copy(g).start())
+        reduce_at(ready, outer, start_outer)
         reduce_at(ready + 4, inner, add_outer)
-        reduce_at(ready + 5, inner, lambda g: middle_copy(g).start())
+        reduce_at(ready + 5, inner, start_middle)
         reduce_at(ready + 9, inner, add_middle)
-        reduce_at(ready + 10, inner, lambda g: total_copy(g).start())
-        reduce_at(ready + 10, inner, flatten)
+        reduce_at(ready + 10, inner, start_total)
         reduce_at(ready + 15, outer, receive)
         lax.fori_loop(prepared(t), prepared(t + 1), plane_step, 0)
         stage_at(2, sum_step)
@@ -578,6 +613,15 @@
         return carry
 
     lax.fori_loop(0, per_layer, plane_step, 0)
+
+    @pl.when(outer)
+    def _():
+        pl.semaphore_wait(barrier, 4)
+
+    @pl.when(inner)
+    def _():
+        pl.semaphore_wait(barrier, 5)
+
     lax.fori_loop(0, last + units, tick, 0)
 
     local_copy.wait()
@@ -644,13 +688,11 @@
             moved = exact_left(qx_ref, jnp.concatenate(scaled, 1))
             for k, i in enumerate(ids):
                 put_rows(lines.at[g], i, moved[:, k * nz : (k + 1) * nz])
-        if g > 0:
-            for k in (2, 3, 1):
-                back_copy(g - 1, k).start()
-    for k in (2, 3, 1):
-        back_copy(share - 1, k).start()
-    for g in range(share):
-        returned[mine + place * share + g] = lines[g, lines_of(place)]
+        row = mine + place * share + g
+        returned[row] = lines[g, lines_of(place)]
+        for k in (2, 1, 3):
+            back_copy(g, k).start()
+        pair_copy(row).start()
     for g in range(share):
         for k in (1, 2, 3):
             line_copy(g, k).wait_send()
@@ -658,8 +700,6 @@
     def straighten(row):
         spectrum[row] = exact_right(returned[row], qzt_ref)
 
-    for g in range(share):
-        pair_copy(mine + place * share + g).start()
     for g in range(share):
         straighten(mine + place * share + g)
     for g in range(share):
@@ -690,13 +730,15 @@
     @pl.when(outer)
     def _():
         for g in range(groups):
-            outer_copy(g).wait_send()
+            for p in range(2):
+                outer_copy(g, p).wait_send()
 
     @pl.when(inner)
     def _():
         for g in range(groups):
-            middle_copy(g).wait_send()
-            total_copy(g).wait_send()
+            for p in range(2):
+                middle_copy(g, p).wait_send()
+                total_copy(g, p).wait_send()
 
     for k in (0, 3, 1, 2):
         for g in range(share):
@@ -725,7 +767,7 @@
     lax.fori_loop(0, groups // 2, settle, 0)
 
 
-def evolve(orbitals, v_local, weights, wz, wy):
+def evolve(orbitals, v_local, occupations, wz, wy):
     layers, _, planes, ny, nz = orbitals.shape
     width_x = 4 * planes
     gather, spread, far_rows, far, near_rows = evolve_tables(width_x, planes)
@@ -770,7 +812,7 @@
             dma((3, 2)),
         ]
         + [dma((units,))] * 8
-        + [dma((groups,))] * 6
+        + [dma((groups, 2))] * 6
         + [dma((groups // 8, 3))] * 4
         + [dma((groups,))] * 2
         + [pltpu.SemaphoreType.DMA],
@@ -780,7 +822,7 @@
         cost_estimate=pl.CostEstimate(
             flops=40 * layers * planes * ny * nz * (ny + nz), bytes_accessed=16 * layers * planes * ny * nz, transcendentals=0
         ),
-    )(weights, jnp.asarray(squares[1]), orbitals, v_local, wz, wy, *map(jnp.asarray, [gather, spread] + tables))
+    )(occupations, jnp.asarray(squares[1]), orbitals, v_local, wz, wy, *map(jnp.asarray, [gather, spread] + tables))
     return evolved.reshape(layers, groups, 2, planes, LANE_ROWS, nz), angle
 
 
@@ -815,7 +857,7 @@
 def turn(evolved, angle):
     layers, groups, _, planes, _, nz = evolved.shape
     ny = groups * LANE_ROWS
-    bx = min(4, planes)
+    bx = min(8, planes)
     field_block = pl.BlockSpec((bx, ny, nz), lambda i: (i, 0, 0))
     return pl.pallas_call(
         turn_kernel,
@@ -826,7 +868,7 @@
         ],
         out_specs=pl.BlockSpec((layers, 2, bx, ny, nz), lambda i: (0, 0, i, 0, 0)),
         out_shape=jax.ShapeDtypeStruct((layers, 2, planes, ny, nz), jnp.float32),
-        compiler_params=pltpu.CompilerParams(vmem_limit_bytes=VMEM_LIMIT),
+        compiler_params=pltpu.CompilerParams(vmem_limit_bytes=63 * 1024 * 1024),
     )(evolved, angle)
 
 
@@ -934,7 +976,6 @@
     wy = jnp.asarray(split_const(left_block(kinetic_matrix(count_y))))
     order = np.arange(2 * width_x).reshape(2, grid_count, planes).transpose(1, 0, 2).reshape(-1)
     wx = jnp.asarray(split_const(left_block(kinetic_matrix(width_x))[order][:, order]))
-    weights = lax.dynamic_slice_in_dim(occupations, lax.axis_index("orb") * layers, layers, 0)
     if (
         grid_count == 4
         and orb_count == 4
@@ -943,8 +984,10 @@
         and count_y % (8 * LANE_ROWS) == 0
         and count_z % 128 == 0
     ):
-        evolved, angle = evolve(orbitals, v_local, weights, wz, wy)
+        evolved, angle = evolve(orbitals, v_local, occupations, wz, wy)
         return turn(evolved, angle)
+
+    weights = lax.dynamic_slice_in_dim(occupations, lax.axis_index("orb") * layers, layers, 0)
 
     exchange = partial(lax.all_to_all, axis_name="grid", split_axis=0, concat_axis=0, tiled=True)
 

time: 198 us -> 190 us (0.960)
  Pallas kernels: 193 us -> 186 us
  local copies, waits for them, and re-layouts: 2.82 us -> 0 us
    pallas_call x1, Pallas kernels: 177 us -> 173 us  [evolve(): pl.pallas_call(partial(evolve_kernel, layers, far_rows, far, near_rows, 3...]
    pallas_call x1, Pallas kernels: 15.4 us -> 13.4 us  [turn(): pl.pallas_call(turn_kernel, grid=(planes // bx,), in_specs=[pl.BlockSpec(...]
where the time goes in v3:
time: 190 us; the launch traced here: 186 us
  Pallas kernels  186 us (98%)
    pallas_call x1, Pallas kernels, evolve(): pl.pallas_call(partial(evolve_kernel, layers, far_rows, far, near_rows, 3...  173 us
    pallas_call x1, Pallas kernels, turn(): pl.pallas_call(turn_kernel, grid=(planes // bx,), in_specs=[pl.BlockSpec(...  13.4 us

profile of v3, /device:TPU:0, one launch (start us, length us, event | category | flops | bytes accessed | tf_op | source)
XLA Modules:
  0.0 186.1 jit_solution(13791736043798190130)
XLA Ops:
  0.0 172.7 %shard_map.145 = (f32[4,16,512,128]{3,2,1,0:T(8,128)}, f32[32,128,128]{2,1,0:T(8,128)}) custom-call(f32[16]{0:T(128)} %weight_ref.1, f32[128]{0:T(128)} %constant.22.clone.wave_ref, f32[4,2,32,128,128]{4,3,2,1,0:T(8,128)} %psi_ref.1, f32[32,128,128]{2,1,0:T(8,128)} %local_ref.1, bf16[2,256,256]{2,1,0:T(8,128)(2,1)} %constant.20.clone.wz_ref, ...), custom_call_target="tpu_custom_call" | custom-call | flops 21474836480 | bytes 33554432 | tf_op jit(solution)/shard_map/pallas_call | solution.py:790
  172.7 13.4 %shard_map.146 = f32[4,2,32,128,128]{4,3,2,1,0:T(8,128)} custom-call(f32[4,16,2,32,8,128]{5,4,3,2,1,0:T(8,128)} %bitcast.1, f32[32,128,128]{2,1,0:T(8,128)} %get-tuple-element.8.angle_ref), custom_call_target="tpu_custom_call" | custom-call | tf_op jit(solution)/shard_map/pallas_call | solution.py:862

commit v4 on v3

--- a/solution.py
+++ b/solution.py
@@ -857,7 +857,7 @@
 def turn(evolved, angle):
     layers, groups, _, planes, _, nz = evolved.shape
     ny = groups * LANE_ROWS
-    bx = min(8, planes)
+    bx = min(16, planes)
     field_block = pl.BlockSpec((bx, ny, nz), lambda i: (i, 0, 0))
     return pl.pallas_call(
         turn_kernel,

time: 190 us -> 189 us (level)
  no operation moved by 1% of the time
where the time goes in v4:
time: 189 us; the launch traced here: 185 us
  Pallas kernels  185 us (98%)
    pallas_call x1, Pallas kernels, evolve(): pl.pallas_call(partial(evolve_kernel, layers, far_rows, far, near_rows, 3...  173 us
    pallas_call x1, Pallas kernels, turn(): pl.pallas_call(turn_kernel, grid=(planes // bx,), in_specs=[pl.BlockSpec(...  12.4 us

profile of v4, /device:TPU:0, one launch (start us, length us, event | category | flops | bytes accessed | tf_op | source)
XLA Modules:
  0.0 185.1 jit_solution(13241136575448188698)
XLA Ops:
  0.0 172.7 %shard_map.145 = (f32[4,16,512,128]{3,2,1,0:T(8,128)}, f32[32,128,128]{2,1,0:T(8,128)}) custom-call(f32[16]{0:T(128)} %weight_ref.1, f32[128]{0:T(128)} %constant.22.clone.wave_ref, f32[4,2,32,128,128]{4,3,2,1,0:T(8,128)} %psi_ref.1, f32[32,128,128]{2,1,0:T(8,128)} %local_ref.1, bf16[2,256,256]{2,1,0:T(8,128)(2,1)} %constant.20.clone.wz_ref, ...), custom_call_target="tpu_custom_call" | custom-call | flops 21474836480 | bytes 33554432 | tf_op jit(solution)/shard_map/pallas_call | solution.py:790
  172.7 12.4 %shard_map.146 = f32[4,2,32,128,128]{4,3,2,1,0:T(8,128)} custom-call(f32[4,16,2,32,8,128]{5,4,3,2,1,0:T(8,128)} %bitcast.1, f32[32,128,128]{2,1,0:T(8,128)} %get-tuple-element.8.angle_ref), custom_call_target="tpu_custom_call" | custom-call | tf_op jit(solution)/shard_map/pallas_call | solution.py:862
